TPU v7x, 32 devices: a 4x4x1 block of a 4x4x8 slice. The times are simulated.
32 devices in a mesh: data: 1 (over z), dap: 32 (over y, x, core).
Axes of the slice: x: 4, y: 4, z: 1, core: 2. Of those that a mesh axis runs over, the one named last changes fastest.
The devices are a block of a 4x4x8 slice.
Arguments:
- extra_msa: bfloat16 [12288, 128, 64], P('data', 'dap')
- extra_mask: int32 [12288, 128], P('data')
- main_msa: bfloat16 [256, 128, 256], P('data', 'dap')
- main_mask: int32 [256, 128], P('data')
- pair_act: float32 [128, 128, 128], P(('data', 'dap'))
- extra_ln_gamma: bfloat16 [64], replicated
- extra_ln_beta: bfloat16 [64], replicated
- extra_w_left: bfloat16 [64, 32], replicated
- extra_b_left: bfloat16 [32], replicated
- extra_w_right: bfloat16 [64, 32], replicated
- extra_b_right: bfloat16 [32], replicated
- extra_w_out: bfloat16 [1024, 128], replicated
- extra_b_out: bfloat16 [128], replicated
- main_ln_gamma: bfloat16 [256], replicated
- main_ln_beta: bfloat16 [256], replicated
- main_w_left: bfloat16 [256, 32], replicated
- main_b_left: bfloat16 [32], replicated
- main_w_right: bfloat16 [256, 32], replicated
- main_b_right: bfloat16 [32], replicated
- main_w_out: bfloat16 [1024, 128], replicated
- main_b_out: bfloat16 [128], replicated
Outputs:
- output 1: float32 [128, 128, 128], P(('data', 'dap'))
- output 2: bfloat16 [12288, 128, 64], P(('data', 'dap'))
- output 3: bfloat16 [256, 128, 256], P(('data', 'dap'))
All inputs are finite; a program needn't handle non-finite values.
Results may differ from a plain program's by a relative error of at most 0.00500583.
Values are sent between devices in bfloat16 or wider.
A program may use at most 768 MiB of HBM per device.

v0:
```python
import jax
import jax.numpy as jnp
from jax import lax
from jax.sharding import PartitionSpec as P

LN_EPS = 1e-5
NORM_EPS = 1e-3


def layer_norm(value_a10, ln_gamma, ln_beta):
    as_float = value_a10.astype(jnp.float32)
    row_mean = jnp.mean(as_float, axis=-1, keepdims=True)
    centered = as_float - row_mean
    row_var = jnp.mean(centered * centered, axis=-1, keepdims=True)
    scaled = centered * lax.rsqrt(row_var + LN_EPS)
    return (scaled * ln_gamma.astype(jnp.float32) + ln_beta.astype(jnp.float32)).astype(jnp.bfloat16)


def project_pair(normed, mask_float, w_left, b_left, w_right, b_right):
    hidden = w_left.shape[1]
    w_both = jnp.concatenate([w_left, w_right], axis=1)
    b_both = jnp.concatenate([b_left, b_right]).astype(jnp.float32)
    both_proj = jnp.einsum('...m,mc->...c', normed, w_both, preferred_element_type=jnp.float32)
    both_proj = ((both_proj + b_both) * mask_float[..., None]).astype(jnp.bfloat16)
    return both_proj[..., :hidden], both_proj[..., hidden:]


def pair_counts(mask_rows, mask_full):
    return jnp.einsum('si,sj->ij', mask_rows.astype(jnp.bfloat16), mask_full.astype(jnp.bfloat16), preferred_element_type=jnp.float32)


def gathered_term(value_a9, mask_full, ln_gamma, ln_beta, w_left, b_left, w_right, b_right, w_out, b_out):
    row_count = value_a9.shape[1]
    hidden = w_left.shape[1]
    row_start = lax.axis_index('dap') * row_count
    mask_rows = lax.dynamic_slice_in_dim(mask_full, row_start, row_count, axis=1)
    normed = layer_norm(value_a9, ln_gamma, ln_beta)
    left_proj, right_proj = project_pair(normed, mask_rows.astype(jnp.float32), w_left, b_left, w_right, b_right)
    right_all = lax.all_gather(right_proj, 'dap', axis=1, tiled=True)
    outer_prod = jnp.einsum('sic,sjd->ijcd', left_proj, right_all, preferred_element_type=jnp.float32).astype(jnp.bfloat16)
    pair_sum = jnp.einsum('ijcd,cdk->ijk', outer_prod, w_out.reshape(hidden, hidden, -1), preferred_element_type=jnp.float32)
    counts = pair_counts(mask_rows, mask_full)
    return (pair_sum + b_out.astype(jnp.float32)) / (NORM_EPS + counts)[:, :, None]


def reduced_term(relaid, mask_full, dap_size, ln_gamma, ln_beta, w_left, b_left, w_right, b_right, w_out, b_out):
    seq_local, res_count, array_b9 = relaid.shape
    hidden = w_left.shape[1]
    row_count = res_count // dap_size
    dap_index = lax.axis_index('dap')
    mask_local = lax.dynamic_slice_in_dim(mask_full, dap_index * seq_local, seq_local, axis=0)
    normed = layer_norm(relaid, ln_gamma, ln_beta)
    left_proj, right_proj = project_pair(normed, mask_local.astype(jnp.float32), w_left, b_left, w_right, b_right)
    left_blocks = jnp.moveaxis(left_proj.reshape(seq_local, dap_size, row_count, hidden), 1, 0)
    w_grid = w_out.reshape(hidden, hidden, -1)

    def block_partial(left_block):
        outer_prod = jnp.einsum('sic,sjd->ijcd', left_block, right_proj, preferred_element_type=jnp.float32).astype(jnp.bfloat16)
        return jnp.einsum('ijcd,cdk->ijk', outer_prod, w_grid, preferred_element_type=jnp.float32).astype(jnp.bfloat16)

    partial_sums = lax.map(block_partial, left_blocks).reshape(res_count, res_count, -1)
    reduced = lax.psum_scatter(partial_sums, 'dap', scatter_dimension=0, tiled=True)
    mask_rows = lax.dynamic_slice_in_dim(mask_full, dap_index * row_count, row_count, axis=1)
    counts = pair_counts(mask_rows, mask_full)
    return (reduced.astype(jnp.float32) + b_out.astype(jnp.float32)) / (NORM_EPS + counts)[:, :, None]


def solution(mesh):
    dap_size = mesh.shape['dap']
    value_a8 = P('data', 'dap', None)
    mask_spec = P('data', None)
    row_spec = P(('data', 'dap'), None, None)

    def local_program(extra_block, extra_mask, main_block, main_mask, pair_rows, extra_ln_gamma, extra_ln_beta, extra_w_left, extra_b_left, extra_w_right, extra_b_right, extra_w_out, extra_b_out, main_ln_gamma, main_ln_beta, main_w_left, main_b_left, main_w_right, main_b_right, main_w_out, main_b_out):
        extra_relaid = lax.all_to_all(extra_block, 'dap', 0, 1, tiled=True)
        extra_term = reduced_term(extra_relaid, extra_mask, dap_size, extra_ln_gamma, extra_ln_beta, extra_w_left, extra_b_left, extra_w_right, extra_b_right, extra_w_out, extra_b_out)
        main_term = gathered_term(main_block, main_mask, main_ln_gamma, main_ln_beta, main_w_left, main_b_left, main_w_right, main_b_right, main_w_out, main_b_out)
        main_relaid = lax.all_to_all(main_block, 'dap', 0, 1, tiled=True)
        return pair_rows + extra_term + main_term, extra_relaid, main_relaid

    in_specs = (value_a8, mask_spec, value_a8, mask_spec, row_spec) + (P(),) * 16
    sharded = jax.shard_map(local_program, mesh=mesh, in_specs=in_specs, out_specs=(row_spec, row_spec, row_spec), check_vma=False)
    return sharded
```

profile of v0, /device:TPU:98, one launch (start us, length us, event | category | flops | bytes accessed | tf_op | source)
XLA Modules:
  0.0 438.7 jit_solution(11062715984821376090)
XLA Ops:
  7.2 18.5 %copy.76 = bf16[12288,4,64]{2,1,0:T(4,128)(2,1)} copy(bf16[12288,4,64]{0,2,1:T(8,128)(2,1)} %param.23) | data formatting | bytes 12582912 | tf_op args[0]
  25.7 24.1 %reshape.113 = bf16[32,2,49152]{2,1,0:T(2,128)(2,1)} reshape(bf16[12288,4,64]{2,1,0:T(4,128)(2,1)} %copy.76) | data formatting | bytes 12582912
  49.9 8.2 %all-to-all-start = ((bf16[32,2,49152]{2,1,0:T(2,128)(2,1)}), bf16[32,2,49152]{2,1,0:T(2,128)(2,1)}, u32[]{:S(2)}, u32[]{:S(2)}) async-start(bf16[32,2,49152]{2,1,0:T(2,128)(2,1)} %reshape.113), calls=%async_computation | async-start | bytes 12582912 | tf_op jit(solution)/shard_map/all_to_all | solution.py:75
  67.1 74.8 %all-to-all-done = bf16[32,2,49152]{2,1,0:T(2,128)(2,1)} async-done(((bf16[32,2,49152]{2,1,0:T(2,128)(2,1)}), bf16[32,2,49152]{2,1,0:T(2,128)(2,1)}, u32[]{:S(2)}, u32[]{:S(2)}) %all-to-all-start) | async-done | bytes 6291488 | tf_op jit(solution)/shard_map/all_to_all | solution.py:75
  141.9 23.4 %reshape.114 = bf16[12288,4,64]{2,1,0:T(4,128)(2,1)} reshape(bf16[32,2,49152]{2,1,0:T(2,128)(2,1)} %all-to-all-done) | data formatting | bytes 12582912
  165.3 14.4 %copy.94 = bf16[32,384,4,64]{1,0,3,2:T(8,128)(2,1)} copy(bf16[32,384,4,64]{3,2,1,0:T(4,128)(2,1)} %bitcast.117) | data formatting | bytes 12582912 | tf_op jit(solution)/shard_map/all_to_all | solution.py:75
  179.7 3.8 convert_reduce_fusion
  186.1 18.0 %copy.95 = bf16[32,384,4,64]{1,3,2,0:T(8,128)(2,1)} copy(bf16[32,384,4,64]{3,2,1,0:T(4,128)(2,1)} %bitcast.118) | data formatting | bytes 12582912 | tf_op jit(solution)/shard_map/all_to_all | solution.py:75
  204.4 8.4 %add_convert_fusion = bf16[384,128,64]{0,2,1:T(8,128)(2,1)} fusion(f32[64]{0:T(128)S(1)} %convert_element_type.93, f32[64]{0:T(128)S(1)} %convert_element_type.92, f32[384,128]{0,1:T(8,128)S(1)} %rsqrt.20, f32[384,128]{0,1:T(8,128)S(1)} %div.31, bf16[32,384,4,64]{1,3,2,0:T(8,128)(2,1)} %copy.95), kind=kLoop, calls=%fused_computation.18 | loop fusion | flops 18874368 | bytes 12976640 | tf_op jit(solution)/shard_map/convert_element_type | solution.py:16
  212.8 9.6 %copy.81 = bf16[384,128,64]{1,2,0:T(8,128)(2,1)} copy(bf16[384,128,64]{0,2,1:T(8,128)(2,1)} %add_convert_fusion) | data formatting | bytes 12582912 | tf_op jit(solution)/shard_map/convert_element_type | solution.py:16
  222.5 4.6 %multiply_convert_fusion = bf16[384,128,64]{1,2,0:T(8,128)(2,1)S(1)} fusion(f32[384,128]{1,0:T(8,128)S(1)} %dynamic-slice_convert_fusion.4, f32[64]{0:T(128)S(1)} %maximum_convert_fusion, bf16[384,128,64]{1,2,0:T(8,128)(2,1)} %copy.81, bf16[64,32]{0,1:T(8,128)(2,1)S(1)} %copy-done.6, bf16[64,32]{0,1:T(8,128)(2,1)S(1)} %copy-done.7), kind=kOutput, calls=%fused_computation.17 | convolution fusion | flops 412106752 | bytes 12787968 | tf_op jit(solution)/shard_map/...m,mc->...c/dot_general | solution.py:23
  229.9 5.5 %copy.82 = bf16[384,128,32]{0,2,1:T(8,128)(2,1)} copy(bf16[384,128,32]{1,2,0:T(8,128)(2,1)} %get-tuple-element.87) | data formatting | bytes 6291456 | tf_op jit(solution)/shard_map/slice | solution.py:25
  238.3 115.1 %while.10 = (s32[]{:T(128)}, bf16[32,4,128,128]{3,2,1,0:T(8,128)(2,1)}, bf16[32,384,4,32]{1,3,2,0:T(8,128)(2,1)}, bf16[384,128,32]{1,0,2:T(8,128)(2,1)}, bf16[32,32,128]{2,0,1:T(8,128)(2,1)}, /*index=5*/s32[]{:T(128)}) while((s32[]{:T(128)}, bf16[32,4,128,128]{3,2,1,0:T(8,128)(2,1)}, bf16[32,384,4,32]{1,3,2,0:T(8,128)(2,1)}, ...), condition=%wide.region_3.4_spmd, body=%wide.region_2.3_spmd.sunk | while | flops 537460736 | bytes 3638341 | solution.py:61
  238.3 3.6 fusion.70
  270.7 3.6 fusion.70
  274.3 3.6 fusion.70
  281.5 3.6 fusion.70
  285.1 3.6 fusion.70
  295.9 3.6 fusion.70
  299.5 3.6 fusion.70
  317.4 3.6 fusion.70
  324.6 3.6 fusion.70
  328.2 3.6 fusion.70
  331.9 3.6 fusion.70
  339.1 3.6 fusion.70
  349.9 3.6 fusion.70
  353.5 7.0 %all-to-all-start.1 = ((bf16[256,4,256]{2,1,0:T(4,128)(2,1)}), bf16[256,4,256]{2,1,0:T(4,128)(2,1)S(1)}, u32[]{:S(2)}, u32[]{:S(2)}) async-start(bf16[256,4,256]{2,1,0:T(4,128)(2,1)} %param.25), calls=%async_computation.2 | async-start | bytes 1048576 | tf_op jit(solution)/shard_map/all_to_all | solution.py:78
  360.7 8.0 %fusion.42 = f32[4,128]{1,0:T(4,128)S(1)} fusion(s32[12288,128]{1,0:T(8,128)} %param.24, s32[]{:T(128)S(6)} %select_n.8), kind=kOutput, calls=%fused_computation.35 | convolution fusion | flops 14205440 | bytes 12584964 | tf_op jit(solution)/shard_map/si,sj->ij/dot_general | solution.py:29
  371.8 4.9 %convert_bitcast_fusion = bf16[4,128,32,32]{2,3,0,1:T(8,128)(2,1)} fusion(bf16[256,128,32]{0,2,1:T(8,128)(2,1)} %all-gather.2.cloned.1.call-done, bf16[256,4,64]{0,2,1:T(8,128)(2,1)S(1)} %copy-done.5), kind=kOutput, calls=%fused_computation.20 | convolution fusion | flops 268959744 | bytes 3211264 | tf_op jit(solution)/shard_map/sic,sjd->ijcd/dot_general | solution.py:40
  376.7 6.9 %copy.87 = bf16[4,128,32,32]{1,3,2,0:T(8,128)(2,1)S(1)} copy(bf16[4,128,32,32]{2,3,0,1:T(8,128)(2,1)} %convert_bitcast_fusion) | data formatting | bytes 2097152 | tf_op jit(solution)/shard_map/convert_element_type | solution.py:40
  383.6 9.6 %copy.89 = bf16[384,128,64]{1,2,0:T(8,128)(2,1)} copy(bf16[384,128,64]{0,2,1:T(8,128)(2,1)} %bitcast.119) | data formatting | bytes 12582912
  393.2 36.6 %reduce-scatter.2.cloned.1.call-done = bf16[4,128,128]{2,1,0:T(8,128)(2,1)} async-done(((bf16[128,128,128]{2,1,0:T(8,128)(2,1)}), bf16[4,128,128]{2,1,0:T(8,128)(2,1)}) %reduce-scatter.2.cloned.1.call-update) | async-done | bytes 131088 | tf_op jit(solution)/shard_map/reduce_scatter | solution.py:62
  (101 shorter events, 91.1 us)
Async XLA Ops:
  7.2 422.6 %copy-start = (bf16[1024,128]{1,0:T(8,128)(2,1)S(1)}, bf16[1024,128]{1,0:T(8,128)(2,1)}, u32[]{:S(2)}) copy-start(bf16[1024,128]{1,0:T(8,128)(2,1)} %param.42) | copy-start | bytes 786436
  49.8 8.3 %copy-start.2 = (s32[256,128]{1,0:T(8,128)S(1)}, s32[256,128]{1,0:T(8,128)}, u32[]{:S(2)}) copy-start(s32[256,128]{1,0:T(8,128)} %param.26) | copy-start | bytes 393220
  49.8 8.5 %copy-start.11 = (bf16[256]{0:T(256)(128)(2,1)S(1)}, bf16[256]{0:T(256)(128)(2,1)}, u32[]{:S(2)}) copy-start(bf16[256]{0:T(256)(128)(2,1)} %param.36) | copy-start | bytes 1540
  49.8 8.6 %copy-start.12 = (bf16[256]{0:T(256)(128)(2,1)S(1)}, bf16[256]{0:T(256)(128)(2,1)}, u32[]{:S(2)}) copy-start(bf16[256]{0:T(256)(128)(2,1)} %param.37) | copy-start | bytes 1540
  49.8 8.6 %copy-start.13 = (bf16[32]{0:T(256)(128)(2,1)S(1)}, bf16[32]{0:T(256)(128)(2,1)}, u32[]{:S(2)}) copy-start(bf16[32]{0:T(256)(128)(2,1)} %param.41) | copy-start | bytes 196
  49.8 8.6 %copy-start.14 = (bf16[32]{0:T(256)(128)(2,1)S(1)}, bf16[32]{0:T(256)(128)(2,1)}, u32[]{:S(2)}) copy-start(bf16[32]{0:T(256)(128)(2,1)} %param.39) | copy-start | bytes 196
  49.8 13.5 %copy-start.9 = (bf16[256,32]{0,1:T(8,128)(2,1)S(1)}, bf16[256,32]{0,1:T(8,128)(2,1)}, u32[]{:S(2)}) copy-start(bf16[256,32]{0,1:T(8,128)(2,1)} %param.40) | copy-start | bytes 49156
  49.8 13.5 %copy-start.10 = (bf16[256,32]{0,1:T(8,128)(2,1)S(1)}, bf16[256,32]{0,1:T(8,128)(2,1)}, u32[]{:S(2)}) copy-start(bf16[256,32]{0,1:T(8,128)(2,1)} %param.38) | copy-start | bytes 49156
  49.8 15.4 %copy-start.15 = (bf16[64]{0:T(256)(128)(2,1)S(1)}, bf16[64]{0:T(256)(128)(2,1)}, u32[]{:S(2)}) copy-start(bf16[64]{0:T(256)(128)(2,1)} %param.28) | copy-start | bytes 388
  49.8 15.4 %copy-start.16 = (bf16[64]{0:T(256)(128)(2,1)S(1)}, bf16[64]{0:T(256)(128)(2,1)}, u32[]{:S(2)}) copy-start(bf16[64]{0:T(256)(128)(2,1)} %param.29) | copy-start | bytes 388
  49.9 15.4 %copy-start.3 = (bf16[1024,128]{1,0:T(8,128)(2,1)S(1)}, bf16[1024,128]{1,0:T(8,128)(2,1)}, u32[]{:S(2)}) copy-start(bf16[1024,128]{1,0:T(8,128)(2,1)} %param.34) | copy-start | bytes 786436
  49.9 16.2 %copy-start.17 = (bf16[32]{0:T(256)(128)(2,1)S(1)}, bf16[32]{0:T(256)(128)(2,1)}, u32[]{:S(2)}) copy-start(bf16[32]{0:T(256)(128)(2,1)} %param.33) | copy-start | bytes 196
  49.9 16.2 %copy-start.18 = (bf16[32]{0:T(256)(128)(2,1)S(1)}, bf16[32]{0:T(256)(128)(2,1)}, u32[]{:S(2)}) copy-start(bf16[32]{0:T(256)(128)(2,1)} %param.31) | copy-start | bytes 196
  49.9 92.0 %all-to-all-start = ((bf16[32,2,49152]{2,1,0:T(2,128)(2,1)}), bf16[32,2,49152]{2,1,0:T(2,128)(2,1)}, u32[]{:S(2)}, u32[]{:S(2)}) async-start(bf16[32,2,49152]{2,1,0:T(2,128)(2,1)} %reshape.113), calls=%async_computation | async-start | bytes 12582912 | tf_op jit(solution)/shard_map/all_to_all | solution.py:75
  58.1 313.7 %all-gather.2.cloned.1.call-start = ((), (), s32[]{:S(2)}) async-start(), calls=%async_computation.4 | async-start | bytes 2162688 | tf_op jit(solution)/shard_map/all_gather | solution.py:39
  63.6 0.7 copy-start.4
  65.0 364.8 %reduce-scatter.2.cloned.1.call-start = ((), (), s32[]{:S(2)}) async-start(), calls=%async_computation.3 | async-start | bytes 4325376 | tf_op jit(solution)/shard_map/reduce_scatter | solution.py:62
  179.7 4.6 %copy-start.1 = (bf16[32,384,4,64]{1,0,3,2:T(8,128)(2,1)S(1)}, bf16[32,384,4,64]{1,0,3,2:T(8,128)(2,1)}, u32[]{:S(2)}) copy-start(bf16[32,384,4,64]{1,0,3,2:T(8,128)(2,1)} %copy.94) | copy-start | bytes 18874372
  212.8 9.6 %copy-start.6 = (bf16[64,32]{0,1:T(8,128)(2,1)S(1)}, bf16[64,32]{0,1:T(8,128)(2,1)}, u32[]{:S(2)}) copy-start(bf16[64,32]{0,1:T(8,128)(2,1)} %param.32) | copy-start | bytes 12292
  212.8 9.6 %copy-start.7 = (bf16[64,32]{0,1:T(8,128)(2,1)S(1)}, bf16[64,32]{0,1:T(8,128)(2,1)}, u32[]{:S(2)}) copy-start(bf16[64,32]{0,1:T(8,128)(2,1)} %param.30) | copy-start | bytes 12292
  238.3 122.2 %copy-start.19 = (bf16[128]{0:T(256)(128)(2,1)S(1)}, bf16[128]{0:T(256)(128)(2,1)}, u32[]{:S(2)}) copy-start(bf16[128]{0:T(256)(128)(2,1)} %param.43) | copy-start | bytes 772
  238.3 122.2 %copy-start.20 = (bf16[128]{0:T(256)(128)(2,1)S(1)}, bf16[128]{0:T(256)(128)(2,1)}, u32[]{:S(2)}) copy-start(bf16[128]{0:T(256)(128)(2,1)} %param.35) | copy-start | bytes 772
  353.5 18.3 %copy-start.5 = (bf16[256,4,64]{0,2,1:T(8,128)(2,1)S(1)}, bf16[256,4,64]{0,2,1:T(8,128)(2,1)}, u32[]{:S(2)}) copy-start(bf16[256,4,64]{0,2,1:T(8,128)(2,1)} %copy-done.4) | copy-start | bytes 393220
  353.5 17.2 %all-to-all-start.1 = ((bf16[256,4,256]{2,1,0:T(4,128)(2,1)}), bf16[256,4,256]{2,1,0:T(4,128)(2,1)S(1)}, u32[]{:S(2)}, u32[]{:S(2)}) async-start(bf16[256,4,256]{2,1,0:T(4,128)(2,1)} %param.25), calls=%async_computation.2 | async-start | bytes 1048576 | tf_op jit(solution)/shard_map/all_to_all | solution.py:78
  383.6 46.2 %copy-start.8 = (f32[4,128,128]{2,1,0:T(8,128)S(1)}, f32[4,128,128]{2,1,0:T(8,128)}, u32[]{:S(2)}) copy-start(f32[4,128,128]{2,1,0:T(8,128)} %param.27) | copy-start | bytes 786436
Sparse Core Ops, SparseCore 0:
  65.1 73.3 all-gather.1
  353.6 76.0 reduce-scatter.1
where the time goes:
time: 442 us; the launch traced here: 439 us
  local copies, waits for them, and re-layouts  140 us (32%)
  matrix products  135 us (31%)
  waiting for transfers between devices  113 us (26%)
  other arithmetic  19.9 us (5%)
  starting transfers between devices  15.5 us (4%)
  between operations  14.5 us (3%)
    dot_general x32, matrix products, block_partial(): jnp.einsum('ijcd,cdk->ijk', outer_prod, w_grid, preferred_element_type=jn...  115 us
    unnamed x47, local copies, waits for them, and re-layouts  77.2 us
    all_to_all x1, waiting for transfers between devices, local_program(): extra_relaid = lax.all_to_all(extra_block, 'dap', 0, 1, tiled=True)  74.8 us
    reduce_scatter x1, waiting for transfers between devices, reduced_term(): lax.psum_scatter(partial_sums, 'dap', scatter_dimension=0, tiled=True)  36.6 us
    all_to_all x2, local copies, waits for them, and re-layouts, local_program(): extra_relaid = lax.all_to_all(extra_block, 'dap', 0, 1, tiled=True)  32.4 us
    convert_element_type x2, other arithmetic, layer_norm(): (scaled * ln_gamma.astype(jnp.float32) + ln_beta.astype(jnp.float32)).ast...  10.1 us
    convert_element_type x1, local copies, waits for them, and re-layouts, layer_norm(): (scaled * ln_gamma.astype(jnp.float32) + ln_beta.astype(jnp.float32)).ast...  9.62 us
    slice x3, local copies, waits for them, and re-layouts, project_pair(): return (both_proj[..., :hidden], both_proj[..., hidden:])  9.03 us
  transfers between devices with their start and end apart: 4, of which 3 were waited for; matrix products, arithmetic and copies ran while one was open for 57% of the time, Pallas kernels for 0%

commit v1 on v0

v1 whole, which is shorter than its diff:
```python
import functools

import jax
import jax.numpy as jnp
from jax import lax
from jax.experimental import pallas as pl
from jax.experimental.pallas import tpu as pltpu
from jax.sharding import PartitionSpec as P

LN_EPS = 1e-5
NORM_EPS = 1e-3
F32 = jnp.float32
BF16 = jnp.bfloat16
MESH_ID = pl.DeviceIdType.MESH
SIDE = 4
CORES = 2
SEND_ORDER = ((1, 1), (3, 3), (1, 3), (3, 1), (1, 2), (3, 2), (1, 0), (3, 0), (2, 2), (0, 2), (2, 1), (2, 3), (0, 1), (2, 0), (0, 3))


def layer_norm(value_a10, ln_gamma, ln_beta):
    as_float = value_a10.astype(jnp.float32)
    row_mean = jnp.mean(as_float, axis=-1, keepdims=True)
    centered = as_float - row_mean
    row_var = jnp.mean(centered * centered, axis=-1, keepdims=True)
    scaled = centered * lax.rsqrt(row_var + LN_EPS)
    return (scaled * ln_gamma.astype(jnp.float32) + ln_beta.astype(jnp.float32)).astype(jnp.bfloat16)


def project_pair(normed, mask_float, w_left, b_left, w_right, b_right):
    hidden = w_left.shape[1]
    w_both = jnp.concatenate([w_left, w_right], axis=1)
    b_both = jnp.concatenate([b_left, b_right]).astype(jnp.float32)
    both_proj = jnp.einsum('...m,mc->...c', normed, w_both, preferred_element_type=jnp.float32)
    both_proj = ((both_proj + b_both) * mask_float[..., None]).astype(jnp.bfloat16)
    return both_proj[..., :hidden], both_proj[..., hidden:]


def pair_counts(mask_rows, mask_full):
    return jnp.einsum('si,sj->ij', mask_rows.astype(jnp.bfloat16), mask_full.astype(jnp.bfloat16), preferred_element_type=jnp.float32)


def gathered_term(value_a9, mask_full, ln_gamma, ln_beta, w_left, b_left, w_right, b_right, w_out, b_out):
    row_count = value_a9.shape[1]
    hidden = w_left.shape[1]
    row_start = lax.axis_index('dap') * row_count
    mask_rows = lax.dynamic_slice_in_dim(mask_full, row_start, row_count, axis=1)
    normed = layer_norm(value_a9, ln_gamma, ln_beta)
    left_proj, right_proj = project_pair(normed, mask_rows.astype(jnp.float32), w_left, b_left, w_right, b_right)
    right_all = lax.all_gather(right_proj, 'dap', axis=1, tiled=True)
    outer_prod = jnp.einsum('sic,sjd->ijcd', left_proj, right_all, preferred_element_type=jnp.float32).astype(jnp.bfloat16)
    pair_sum = jnp.einsum('ijcd,cdk->ijk', outer_prod, w_out.reshape(hidden, hidden, -1), preferred_element_type=jnp.float32)
    counts = pair_counts(mask_rows, mask_full)
    return (pair_sum + b_out.astype(jnp.float32)) / (NORM_EPS + counts)[:, :, None]


def extra_kernel(x_hbm, mask_hbm, z_ref, akron, bkron, gam, bet, ba, bb, wt, bo,
                 xout_hbm, out_ref,
                 xb, xn, aown, apart, bown, bpart, astage, osc, rsend, rrecv, mraw, maskt, counts,
                 xs_sem, xr_sem, xo_sem, ms_sem, as_sem, ar_sem, bs_sem, br_sem, rs_sem, rr_sem):
    me = lax.axis_index('dap')
    core = me % CORES
    chip = me // CORES
    cy = chip // SIDE
    cx = chip % SIDE
    rows, chan, seqs = xb.shape[0] // (SIDE * SIDE * CORES), xb.shape[1], xb.shape[2]
    hidden = bown.shape[0]

    def device(dy, dx, dc):
        return (((cy + dy) % SIDE) * SIDE + (cx + dx) % SIDE) * CORES + (core + dc) % CORES

    barrier = pltpu.get_barrier_semaphore()

    def greet(k, _):
        pl.semaphore_signal(barrier, inc=1, device_id={'dap': (me + k) % (SIDE * SIDE * CORES)}, device_id_type=MESH_ID)
        return 0

    lax.fori_loop(1, SIDE * SIDE * CORES, greet, 0)
    mask_copy = pltpu.make_async_copy(mask_hbm, mraw, ms_sem)
    mask_copy.start()
    own = pl.ds(pl.multiple_of(me * rows, rows), rows)

    def cols(p):
        return pl.ds(pl.multiple_of(p * seqs, 128), seqs)

    pltpu.make_async_copy(x_hbm.at[:, :, cols(me)], xb.at[own], xr_sem.at[0]).start()
    pl.semaphore_wait(barrier, SIDE * SIDE * CORES - 1)

    def x_copy(dy, dx, dc):
        p = device(dy, dx, dc)
        k = (dy * SIDE + dx) * CORES + dc
        return pltpu.make_async_remote_copy(src_ref=x_hbm.at[:, :, cols(p)], dst_ref=xb.at[own], send_sem=xs_sem.at[k], recv_sem=xr_sem.at[k],
                                            device_id={'dap': p}, device_id_type=MESH_ID)

    x_copy(0, 0, 1).start()
    for dy, dx in SEND_ORDER:
        for dc in range(CORES):
            x_copy(dy, dx, dc).start()

    mask_copy.wait()
    counts[...] = jnp.zeros_like(counts)

    def count_step(k, _):
        block = mraw[pl.ds(pl.multiple_of(k * seqs, seqs), seqs), :].astype(F32)
        counts[...] += jnp.dot(block.T.astype(BF16), block.astype(BF16), preferred_element_type=F32)
        return 0

    lax.fori_loop(0, mraw.shape[0] // seqs, count_step, 0)
    maskt[...] = mraw[pl.ds(pl.multiple_of(me * seqs, seqs), seqs), :].astype(F32).T

    partner = device(0, 0, 1)
    chip_rows = rows * CORES
    pair_rows = 2 * chip_rows

    def a_copy(u):
        return pltpu.make_async_remote_copy(src_ref=astage.at[pl.ds(2 * u, 2)], dst_ref=apart.at[pl.ds(2 * u, 2)], send_sem=as_sem.at[u], recv_sem=ar_sem.at[u],
                                            device_id={'dap': partner}, device_id_type=MESH_ID)

    def b_copy(u):
        at = pl.ds(pl.multiple_of(u * pair_rows, pair_rows), pair_rows)
        return pltpu.make_async_remote_copy(src_ref=bown.at[:, at], dst_ref=bpart.at[:, at], send_sem=bs_sem.at[u], recv_sem=br_sem.at[u],
                                            device_id={'dap': partner}, device_id_type=MESH_ID)

    def xout_copy(u):
        at = pl.ds(pl.multiple_of(u * pair_rows, pair_rows), pair_rows)
        return pltpu.make_async_copy(xb.at[at], xout_hbm.at[at], xo_sem.at[u])

    def unit_step(pos, _):
        late = pos // 4
        dy = (1 - late) * (1 + 2 * (pos % 2)) + late * (2 - 2 * (pos % 2))
        half = (cx // 2 + 1 - (pos // 2) % 2) % 2
        ysrc = (cy - dy + SIDE) % SIDE
        u = ysrc * 2 + half
        for xx in range(2):
            dx = (cx - (2 * half + xx) + SIDE) % SIDE
            for dc in range(CORES):
                k = (dy * SIDE + dx) * CORES + dc
                pltpu.make_async_remote_copy(src_ref=xb.at[own], dst_ref=xb.at[own], send_sem=xs_sem.at[k], recv_sem=xr_sem.at[k],
                                             device_id={'dap': partner}, device_id_type=MESH_ID).wait_recv()
        xout_copy(u).start()

        def norm_step(n, _):
            for lt in range(seqs // 128):
                ls = pl.ds(lt * 128, 128)
                v = xb[u * pair_rows + n, :, ls].astype(F32)
                mean = jnp.sum(v, axis=0, keepdims=True) * (1.0 / chan)
                d = v - mean
                var = jnp.sum(d * d, axis=0, keepdims=True) * (1.0 / chan)
                xn[pl.ds(pl.multiple_of(n * chan, chan), chan), ls] = (d * lax.rsqrt(var + LN_EPS) * gam[...] + bet[...]).astype(BF16)
            return 0

        lax.fori_loop(0, pair_rows, norm_step, 0)
        for k in range(2):
            for dst, cc in ((aown, core), (astage, (core + 1) % CORES)):
                r0 = k * chip_rows + cc * rows
                acc = jnp.dot(akron[...], xn[pl.ds(pl.multiple_of(r0 * chan, rows * chan), rows * chan), :], preferred_element_type=F32)
                for r in range(rows):
                    m = maskt[pl.ds(u * pair_rows + r0 + r, 1), :]
                    for lt in range(seqs // 128):
                        ls = slice(lt * 128, lt * 128 + 128)
                        part = (acc[r * hidden:(r + 1) * hidden, ls] + ba[...]) * m[:, ls]
                        dst[2 * u + k, pl.ds(r * hidden, hidden), pl.ds(lt * 128, 128)] = part.astype(BF16)
        a_copy(u).start()
        qc = 16
        for q0 in range(0, hidden, qc):
            parts = []
            for k in range(2):
                acc = jnp.dot(bkron[pl.ds(q0 * chip_rows, qc * chip_rows), :], xn[pl.ds(k * chip_rows * chan, chip_rows * chan), :], preferred_element_type=F32)
                m = maskt[pl.ds(pl.multiple_of(u * pair_rows + k * chip_rows, chip_rows), chip_rows), :]
                bias = bb[pl.ds(q0 * chip_rows, qc * chip_rows), :]
                bias = jnp.concatenate([bias] * (seqs // 128), axis=1)
                parts.append((acc + bias).reshape(qc, chip_rows, seqs) * m[None])
            both = jnp.concatenate(parts, axis=1).astype(BF16)
            bown[pl.ds(q0, qc), pl.ds(pl.multiple_of(u * pair_rows, pair_rows), pair_rows), :] = both
        b_copy(u).start()
        return 0

    lax.fori_loop(0, 8, unit_step, 0)

    def exch_wait(u, _):
        a_copy(u).wait()
        b_copy(u).wait()
        xout_copy(u).wait()
        return 0

    lax.fori_loop(0, 8, exch_wait, 0)

    qn = 4
    res = bown.shape[1]

    def block_step(b, _):
        half = (cx // 2 + 1 - b % 2) % 2
        dys = (1 + b // 2, 3 - 3 * (b // 2))
        starts = [((cy + dy) % SIDE) * SIDE + 2 * half for dy in dys]

        def q_step(qt, _):
            lhs = jnp.concatenate([jnp.concatenate([ref[pl.ds(t, 2)].reshape(2 * rows * hidden, seqs) for t in starts], axis=0) for ref in (aown, apart)], axis=1)
            rhs = jnp.concatenate([ref[pl.ds(qt * qn, qn)].reshape(qn * res, seqs) for ref in (bown, bpart)], axis=1)
            prod = lax.dot_general(lhs, rhs, (((1,), (1,)), ((), ())), preferred_element_type=F32).astype(BF16)
            for i in range(4 * rows):
                for q in range(qn):
                    osc[i, pl.ds(pl.multiple_of(qt * (qn * hidden) + q * hidden, hidden), hidden), :] = prod[i * hidden:(i + 1) * hidden, q * res:(q + 1) * res]
            return 0

        lax.fori_loop(0, hidden // qn, q_step, 0)
        for c4 in range(4):
            t = starts[c4 // 2] + c4 % 2
            for r in range(0, rows, 2):
                i = c4 * rows + r
                rhs = jnp.concatenate([osc[i], osc[i + 1]], axis=1)
                pair = jnp.dot(wt[...], rhs, preferred_element_type=F32).astype(BF16)
                rsend[t, r] = pair[:, :res]
                rsend[t, r + 1] = pair[:, res:]
            dy = dys[c4 // 2]
            dx = (t % SIDE - cx + SIDE) % SIDE
            slot = dy * SIDE + dx

            @pl.when(slot != 0)
            def _():
                pltpu.make_async_remote_copy(src_ref=rsend.at[t], dst_ref=rrecv.at[slot], send_sem=rs_sem.at[slot], recv_sem=rr_sem.at[slot],
                                             device_id={'dap': t * CORES + core}, device_id_type=MESH_ID).start()
        return 0

    lax.fori_loop(0, 4, block_step, 0)

    def r_wait(slot, _):
        pltpu.make_async_remote_copy(src_ref=rsend.at[0], dst_ref=rrecv.at[slot], send_sem=rs_sem.at[slot], recv_sem=rr_sem.at[slot],
                                     device_id={'dap': partner}, device_id_type=MESH_ID).wait()
        return 0

    lax.fori_loop(1, SIDE * SIDE, r_wait, 0)
    for r in range(rows):
        acc = lax.fori_loop(1, SIDE * SIDE, lambda s, a: a + rrecv[s, r].astype(F32), rsend[chip, r].astype(F32))
        term = (acc + bo[...]) / (NORM_EPS + counts[pl.ds(me * rows + r, 1), :])
        out_ref[r] = z_ref[r] + term.T

    def x_wait(k, _):
        pltpu.make_async_remote_copy(src_ref=x_hbm.at[:, :, cols(me)], dst_ref=xb.at[own], send_sem=xs_sem.at[k], recv_sem=xr_sem.at[k],
                                     device_id={'dap': partner}, device_id_type=MESH_ID).wait_send()
        return 0

    lax.fori_loop(1, SIDE * SIDE * CORES, x_wait, 0)


def extra_call(x, mask, z, ln_gamma, ln_beta, w_left, b_left, w_right, b_right, w_out, b_out):
    rows, chan, total = x.shape
    devices = SIDE * SIDE * CORES
    res = rows * devices
    seqs = total // devices
    hidden = w_left.shape[1]
    width = w_out.shape[1]
    chip_rows = rows * CORES
    eye_a = jnp.eye(rows, dtype=BF16)
    eye_b = jnp.eye(chip_rows, dtype=BF16)
    akron = (eye_a[:, None, :, None] * w_left.T[None, :, None, :]).reshape(rows * hidden, rows * chan)
    bkron = (w_right.T[:, None, None, :] * eye_b[None, :, :, None]).reshape(hidden * chip_rows, chip_rows * chan)
    lanes = lambda v: jnp.broadcast_to(v.astype(F32)[:, None], (v.shape[0], 128))
    gam, bet, ba = lanes(ln_gamma), lanes(ln_beta), lanes(b_left)
    bb = lanes(jnp.repeat(b_right, chip_rows))
    bo = lanes(b_out)
    wt = w_out.reshape(hidden, hidden, width).transpose(2, 1, 0).reshape(width, hidden * hidden)
    vm = pl.BlockSpec(memory_space=pltpu.VMEM)
    hb = pl.BlockSpec(memory_space=pl.ANY)
    dma = pltpu.SemaphoreType.DMA
    flops = 2 * (total // 16) * (res // 2) * hidden * res * hidden
    return pl.pallas_call(
        extra_kernel,
        out_shape=(jax.ShapeDtypeStruct((res, chan, seqs), BF16), jax.ShapeDtypeStruct(z.shape, F32)),
        in_specs=[hb, hb] + [vm] * 9,
        out_specs=(hb, vm),
        scratch_shapes=[
            pltpu.VMEM((res, chan, seqs), BF16),
            pltpu.VMEM((2 * chip_rows * chan, seqs), BF16),
            pltpu.VMEM((16, rows * hidden, seqs), BF16),
            pltpu.VMEM((16, rows * hidden, seqs), BF16),
            pltpu.VMEM((hidden, res, seqs), BF16),
            pltpu.VMEM((hidden, res, seqs), BF16),
            pltpu.VMEM((16, rows * hidden, seqs), BF16),
            pltpu.VMEM((4 * rows, hidden * hidden, res), BF16),
            pltpu.VMEM((16, rows, width, res), BF16),
            pltpu.VMEM((16, rows, width, res), BF16),
            pltpu.VMEM((total, res), jnp.int32),
            pltpu.VMEM((res, seqs), F32),
            pltpu.VMEM((res, res), F32),
            dma((devices,)), dma((devices,)), dma((8,)), dma, dma((8,)), dma((8,)), dma((8,)), dma((8,)), dma((16,)), dma((16,)),
        ],
        compiler_params=pltpu.CompilerParams(collective_id=0, has_side_effects=True, vmem_limit_bytes=60 * 1024 * 1024),
        cost_estimate=pl.CostEstimate(flops=flops, bytes_accessed=20_000_000, transcendentals=0),
        name='extra_opm',
    )(x, mask, z, akron, bkron, gam, bet, ba, bb, wt, bo)


def solution(mesh):
    value_a8 = P('data', 'dap', None)
    mask_spec = P('data', None)
    row_spec = P(('data', 'dap'), None, None)

    def local_program(extra_block, extra_mask, main_block, main_mask, pair_rows, extra_ln_gamma, extra_ln_beta, extra_w_left, extra_b_left, extra_w_right, extra_b_right, extra_w_out, extra_b_out, main_ln_gamma, main_ln_beta, main_w_left, main_b_left, main_w_right, main_b_right, main_w_out, main_b_out):
        relaid, summed = extra_call(extra_block.transpose(1, 2, 0), extra_mask, pair_rows, extra_ln_gamma, extra_ln_beta, extra_w_left, extra_b_left, extra_w_right, extra_b_right, extra_w_out, extra_b_out)
        extra_relaid = relaid.transpose(2, 0, 1)
        main_term = gathered_term(main_block, main_mask, main_ln_gamma, main_ln_beta, main_w_left, main_b_left, main_w_right, main_b_right, main_w_out, main_b_out)
        main_relaid = lax.all_to_all(main_block, 'dap', 0, 1, tiled=True)
        return summed + main_term, extra_relaid, main_relaid

    in_specs = (value_a8, mask_spec, value_a8, mask_spec, row_spec) + (P(),) * 16
    return jax.shard_map(local_program, mesh=mesh, in_specs=in_specs, out_specs=(row_spec, row_spec, row_spec), check_vma=False)
```

time: 442 us -> 194 us (0.44)
  Pallas kernels: 0 us -> 128 us
  matrix products: 135 us -> 7.13 us
  local copies, waits for them, and re-layouts: 140 us -> 25.9 us
  waiting for transfers between devices: 113 us -> 0.06 us
  other arithmetic: 19.9 us -> 7.19 us
  starting transfers between devices: 15.5 us -> 8.24 us
    pallas_call x0 -> x1, Pallas kernels: none -> 128 us  [extra_call(): pl.pallas_call(extra_kernel, out_shape=(jax.ShapeDtypeStruct((res, chan,...]
    dot_general x32 -> x0, matrix products: 115 us -> none  [block_partial(): jnp.einsum('ijcd,cdk->ijk', outer_prod, w_grid, preferred_element_type=jn...]
    all_to_all x1 -> x0, waiting for transfers between devices: 74.8 us -> none  [local_program(): extra_relaid = lax.all_to_all(extra_block, 'dap', 0, 1, tiled=True)]
    unnamed x47 -> x26, local copies, waits for them, and re-layouts: 77.2 us -> 9.73 us
    reduce_scatter x1 -> x0, waiting for transfers between devices: 36.6 us -> none  [reduced_term(): lax.psum_scatter(partial_sums, 'dap', scatter_dimension=0, tiled=True)]
    all_to_all x2 -> x0, local copies, waits for them, and re-layouts: 32.4 us -> none  [local_program(): extra_relaid = lax.all_to_all(extra_block, 'dap', 0, 1, tiled=True)]
    convert_element_type x1, local copies, waits for them, and re-layouts: 9.62 us -> 0.09 us  [extra_call(): v.astype(F32)[:, None]]
    convert_element_type x2 -> x1, other arithmetic: 10.1 us -> 1.66 us  [layer_norm(): (scaled * ln_gamma.astype(jnp.float32) + ln_beta.astype(jnp.float32)).ast...]
  transfers between devices with their start and end apart: 4 -> 2, of which waited for: 3 -> 0; matrix products, arithmetic and copies ran while one was open for 57% -> 9% of each run, Pallas kernels for 0% -> 67%
where the time goes in v1:
time: 194 us; the launch traced here: 190 us
  Pallas kernels  128 us (66%)
  local copies, waits for them, and re-layouts  25.9 us (13%)
  between operations  14.3 us (7%)
  starting transfers between devices  8.24 us (4%)
  other arithmetic  7.19 us (4%)
  matrix products  7.13 us (4%)
    pallas_call x1, Pallas kernels, extra_call(): pl.pallas_call(extra_kernel, out_shape=(jax.ShapeDtypeStruct((res, chan,...  128 us
    unnamed x26, local copies, waits for them, and re-layouts  9.73 us
    all_to_all x1, starting transfers between devices, local_program(): main_relaid = lax.all_to_all(main_block, 'dap', 0, 1, tiled=True)  8.18 us
    convert_element_type x1, local copies, waits for them, and re-layouts, gathered_term(): jnp.einsum('sic,sjd->ijcd', left_proj, right_all, preferred_element_type=...  6.97 us
    dot_general x1, matrix products, gathered_term(): jnp.einsum('sic,sjd->ijcd', left_proj, right_all, preferred_element_type=...  4.8 us
  transfers between devices with their start and end apart: 2, of which 0 were waited for; matrix products, arithmetic and copies ran while one was open for 9% of the time, Pallas kernels for 67%

profile of v1, /device:TPU:98, one launch (start us, length us, event | category | flops | bytes accessed | tf_op | source)
XLA Modules:
  0.0 190.4 jit_solution(234691479664766205)
XLA Ops:
  7.3 1.0 constant_dynamic-slice_fusion
  8.4 0.1 copy.57
  8.5 1.4 convert_reduce_fusion
  9.9 1.8 fusion.8
  11.7 0.7 convert_element_type.86
  12.4 0.7 convert_element_type.87
  13.0 0.7 maximum_convert_fusion
  13.8 1.7 fusion.11
  15.5 1.0 fusion.7
  16.5 0.6 slice.8
  17.2 8.2 %all-to-all-start = ((bf16[256,4,256]{2,1,0:T(4,128)(2,1)}), bf16[256,4,256]{2,1,0:T(4,128)(2,1)S(1)}, u32[]{:S(2)}, u32[]{:S(2)}) async-start(bf16[256,4,256]{2,1,0:T(4,128)(2,1)} %param.23), calls=%async_computation | async-start | bytes 1048576 | tf_op jit(solution)/shard_map/all_to_all | solution.py:301
  25.4 0.1 broadcast_multiply_fusion
  25.5 1.0 mul.71.bkron
  26.5 0.1 copy.48
  26.6 0.9 copy.49.wt
  27.5 0.1 broadcast_multiply_fusion.2
  27.6 0.8 mul.67.akron
  28.4 0.1 broadcast_in_dim.15
  28.5 0.1 convert_element_type.83
  28.6 0.8 broadcast_in_dim.16.bb
  29.3 0.7 broadcast_in_dim.17.bo
  30.0 0.7 broadcast_in_dim.12.gam
  30.7 0.7 broadcast_in_dim.13.bet
  31.4 0.7 broadcast_in_dim.14.ba
  32.1 127.6 %extra_opm.1 = (bf16[128,64,384]{2,1,0:T(8,128)(2,1)}, f32[4,128,128]{2,1,0:T(8,128)}) custom-call(bf16[4,64,12288]{2,1,0:T(8,128)(2,1)} %bitcast.49, s32[12288,128]{1,0:T(8,128)} %mask_hbm.1, f32[4,128,128]{2,1,0:T(8,128)} %z_ref.1, bf16[128,256]{1,0:T(8,128)(2,1)} %mul.67.akron, bf16[256,512]{1,0:T(8,128)(2,1)} %mul.71.bkron, ...), custom_call_target="tpu_custom_call" | custom-call | flops 12884901888 | bytes 20000000 | tf_op jit(solution)/shard_map/extra_opm/pallas_call | solution.py:265
  159.7 9.6 %copy.54 = bf16[384,128,64]{1,2,0:T(8,128)(2,1)} copy(bf16[384,128,64]{0,2,1:T(8,128)(2,1)} %bitcast.42) | data formatting | bytes 12582912
  169.3 0.1 convolution_add_fusion.1
  169.4 0.2 copy.61
  169.6 0.9 all_to_all.16
  170.5 4.8 %convert_bitcast_fusion = bf16[4,128,32,32]{2,3,0,1:T(8,128)(2,1)} fusion(bf16[256,128,32]{0,2,1:T(8,128)(2,1)} %all-gather.2.cloned.1.call-done, bf16[256,4,64]{0,2,1:T(8,128)(2,1)S(1)} %fusion.7), kind=kOutput, calls=%fused_computation | convolution fusion | flops 268959744 | bytes 3211264 | tf_op jit(solution)/shard_map/sic,sjd->ijcd/dot_general | solution.py:50
  175.3 7.0 %copy.52 = bf16[4,128,32,32]{1,3,2,0:T(8,128)(2,1)S(1)} copy(bf16[4,128,32,32]{2,3,0,1:T(8,128)(2,1)} %convert_bitcast_fusion) | data formatting | bytes 2097152 | tf_op jit(solution)/shard_map/convert_element_type | solution.py:50
  182.3 1.2 fusion.6
  (34 shorter events, 0.2 us)
Async XLA Ops:
  7.2 175.2 %copy-start = (bf16[1024,128]{1,0:T(8,128)(2,1)S(1)}, bf16[1024,128]{1,0:T(8,128)(2,1)}, u32[]{:S(2)}) copy-start(bf16[1024,128]{1,0:T(8,128)(2,1)} %param.40) | copy-start | bytes 786436
  7.2 18.2 %copy-start.3 = (bf16[64,32]{0,1:T(8,128)(2,1)S(1)}, bf16[64,32]{0,1:T(8,128)(2,1)}, u32[]{:S(2)}) copy-start(bf16[64,32]{0,1:T(8,128)(2,1)} %param.30) | copy-start | bytes 12292
  7.2 19.3 %copy-start.2 = (bf16[1024,128]{1,0:T(8,128)(2,1)S(1)}, bf16[1024,128]{1,0:T(8,128)(2,1)}, u32[]{:S(2)}) copy-start(bf16[1024,128]{1,0:T(8,128)(2,1)} %param.32) | copy-start | bytes 786436
  7.2 20.3 %copy-start.4 = (bf16[64,32]{0,1:T(8,128)(2,1)S(1)}, bf16[64,32]{0,1:T(8,128)(2,1)}, u32[]{:S(2)}) copy-start(bf16[64,32]{0,1:T(8,128)(2,1)} %param.28) | copy-start | bytes 12292
  7.2 163.3 %all-gather.2.cloned.1.call-start = ((), (), s32[]{:S(2)}) async-start(), calls=%async_computation.1 | async-start | bytes 2162688 | tf_op jit(solution)/shard_map/all_gather | solution.py:49
  8.3 20.0 %copy-start.8 = (bf16[32]{0:T(256)(128)(2,1)S(1)}, bf16[32]{0:T(256)(128)(2,1)}, u32[]{:S(2)}) copy-start(bf16[32]{0:T(256)(128)(2,1)} %param.31) | copy-start | bytes 196
  8.4 20.9 %copy-start.5 = (bf16[128]{0:T(256)(128)(2,1)S(1)}, bf16[128]{0:T(256)(128)(2,1)}, u32[]{:S(2)}) copy-start(bf16[128]{0:T(256)(128)(2,1)} %param.33) | copy-start | bytes 772
  8.4 21.6 %copy-start.6 = (bf16[64]{0:T(256)(128)(2,1)S(1)}, bf16[64]{0:T(256)(128)(2,1)}, u32[]{:S(2)}) copy-start(bf16[64]{0:T(256)(128)(2,1)} %param.26) | copy-start | bytes 388
  8.4 22.3 %copy-start.7 = (bf16[64]{0:T(256)(128)(2,1)S(1)}, bf16[64]{0:T(256)(128)(2,1)}, u32[]{:S(2)}) copy-start(bf16[64]{0:T(256)(128)(2,1)} %param.27) | copy-start | bytes 388
  8.5 23.0 %copy-start.9 = (bf16[32]{0:T(256)(128)(2,1)S(1)}, bf16[32]{0:T(256)(128)(2,1)}, u32[]{:S(2)}) copy-start(bf16[32]{0:T(256)(128)(2,1)} %param.29) | copy-start | bytes 196
  17.2 152.2 %all-to-all-start = ((bf16[256,4,256]{2,1,0:T(4,128)(2,1)}), bf16[256,4,256]{2,1,0:T(4,128)(2,1)S(1)}, u32[]{:S(2)}, u32[]{:S(2)}) async-start(bf16[256,4,256]{2,1,0:T(4,128)(2,1)} %param.23), calls=%async_computation | async-start | bytes 1048576 | tf_op jit(solution)/shard_map/all_to_all | solution.py:301
  32.1 127.6 %copy-start.10 = (bf16[128]{0:T(256)(128)(2,1)S(1)}, bf16[128]{0:T(256)(128)(2,1)}, u32[]{:S(2)}) copy-start(bf16[128]{0:T(256)(128)(2,1)} %param.41) | copy-start | bytes 772
  159.7 9.6 %copy-start.1 = (s32[256,128]{1,0:T(8,128)S(1)}, s32[256,128]{1,0:T(8,128)}, u32[]{:S(2)}) copy-start(s32[256,128]{1,0:T(8,128)} %param.24) | copy-start | bytes 393220
  175.3 7.0 %copy-start.11 = (f32[4,128,128]{2,1,0:T(8,128)S(1)}, f32[4,128,128]{2,1,0:T(8,128)}, u32[]{:S(2)}) copy-start(f32[4,128,128]{2,1,0:T(8,128)} %get-tuple-element.5) | copy-start | bytes 786436
Sparse Core Ops, SparseCore 0:
  17.3 82.4 all-gather.1

commit v2 on v1

--- a/solution.py
+++ b/solution.py
@@ -17,46 +17,13 @@
 SEND_ORDER = ((1, 1), (3, 3), (1, 3), (3, 1), (1, 2), (3, 2), (1, 0), (3, 0), (2, 2), (0, 2), (2, 1), (2, 3), (0, 1), (2, 0), (0, 3))
 
 
-def layer_norm(value_a10, ln_gamma, ln_beta):
-    as_float = value_a10.astype(jnp.float32)
-    row_mean = jnp.mean(as_float, axis=-1, keepdims=True)
-    centered = as_float - row_mean
-    row_var = jnp.mean(centered * centered, axis=-1, keepdims=True)
-    scaled = centered * lax.rsqrt(row_var + LN_EPS)
-    return (scaled * ln_gamma.astype(jnp.float32) + ln_beta.astype(jnp.float32)).astype(jnp.bfloat16)
-
-
-def project_pair(normed, mask_float, w_left, b_left, w_right, b_right):
-    hidden = w_left.shape[1]
-    w_both = jnp.concatenate([w_left, w_right], axis=1)
-    b_both = jnp.concatenate([b_left, b_right]).astype(jnp.float32)
-    both_proj = jnp.einsum('...m,mc->...c', normed, w_both, preferred_element_type=jnp.float32)
-    both_proj = ((both_proj + b_both) * mask_float[..., None]).astype(jnp.bfloat16)
-    return both_proj[..., :hidden], both_proj[..., hidden:]
-
-
-def pair_counts(mask_rows, mask_full):
-    return jnp.einsum('si,sj->ij', mask_rows.astype(jnp.bfloat16), mask_full.astype(jnp.bfloat16), preferred_element_type=jnp.float32)
-
-
-def gathered_term(value_a9, mask_full, ln_gamma, ln_beta, w_left, b_left, w_right, b_right, w_out, b_out):
-    row_count = value_a9.shape[1]
-    hidden = w_left.shape[1]
-    row_start = lax.axis_index('dap') * row_count
-    mask_rows = lax.dynamic_slice_in_dim(mask_full, row_start, row_count, axis=1)
-    normed = layer_norm(value_a9, ln_gamma, ln_beta)
-    left_proj, right_proj = project_pair(normed, mask_rows.astype(jnp.float32), w_left, b_left, w_right, b_right)
-    right_all = lax.all_gather(right_proj, 'dap', axis=1, tiled=True)
-    outer_prod = jnp.einsum('sic,sjd->ijcd', left_proj, right_all, preferred_element_type=jnp.float32).astype(jnp.bfloat16)
-    pair_sum = jnp.einsum('ijcd,cdk->ijk', outer_prod, w_out.reshape(hidden, hidden, -1), preferred_element_type=jnp.float32)
-    counts = pair_counts(mask_rows, mask_full)
-    return (pair_sum + b_out.astype(jnp.float32)) / (NORM_EPS + counts)[:, :, None]
-
-
-def extra_kernel(x_hbm, mask_hbm, z_ref, akron, bkron, gam, bet, ba, bb, wt, bo,
-                 xout_hbm, out_ref,
-                 xb, xn, aown, apart, bown, bpart, astage, osc, rsend, rrecv, mraw, maskt, counts,
-                 xs_sem, xr_sem, xo_sem, ms_sem, as_sem, ar_sem, bs_sem, br_sem, rs_sem, rr_sem):
+def opm_kernel(x_hbm, mask_hbm, main_hbm, z_ref, akron, bkron, gam, bet, ba, bb, wt, bo,
+               main_ref, mmask, mgam, mbet, mw, mbias, mwt, mbo,
+               xout_hbm, out_ref, mout_hbm,
+               xb, xn, aown, apart, bown, bpart, astage, osc, rsend, rrecv, mraw, maskt, counts,
+               mrows, am, perm, gall, bm, rmain, mmaskt, mcounts,
+               xs_sem, xr_sem, xo_sem, ms_sem, as_sem, ar_sem, bs_sem, br_sem, rs_sem, rr_sem,
+               cs_sem, cr_sem, gs_sem, gr_sem):
     me = lax.axis_index('dap')
     core = me % CORES
     chip = me // CORES
@@ -91,10 +58,68 @@
         return pltpu.make_async_remote_copy(src_ref=x_hbm.at[:, :, cols(p)], dst_ref=xb.at[own], send_sem=xs_sem.at[k], recv_sem=xr_sem.at[k],
                                             device_id={'dap': p}, device_id_type=MESH_ID)
 
+    mseqs = mout_hbm.shape[0]
+    mtotal = main_ref.shape[0]
+
+    def main_copy(dy, dx, dc):
+        p = device(dy, dx, dc)
+        k = (dy * SIDE + dx) * CORES + dc
+        return pltpu.make_async_remote_copy(src_ref=main_hbm.at[pl.ds(p * mseqs, mseqs)], dst_ref=mout_hbm.at[:, me], send_sem=cs_sem.at[k], recv_sem=cr_sem.at[k],
+                                            device_id={'dap': p}, device_id_type=MESH_ID)
+
+    def send(order):
+        for dy, dx in order:
+            for dc in range(CORES):
+                x_copy(dy, dx, dc).start()
+                main_copy(dy, dx, dc).start()
+
     x_copy(0, 0, 1).start()
-    for dy, dx in SEND_ORDER:
-        for dc in range(CORES):
-            x_copy(dy, dx, dc).start()
+    main_copy(0, 0, 1).start()
+    pltpu.make_async_copy(main_hbm.at[pl.ds(me * mseqs, mseqs)], mout_hbm.at[:, me], cr_sem.at[0]).start()
+    send(SEND_ORDER[:4])
+
+    mmaskt[...] = mmask[...].astype(F32).T
+    mcounts[...] = jnp.dot(mmaskt[...].astype(BF16), mmask[...].astype(F32).astype(BF16), preferred_element_type=F32)
+    mchan = main_ref.shape[2]
+    for st in range(0, mtotal, 32):
+        flat = main_ref[pl.ds(st, 32)].astype(F32).reshape(32 * rows, mchan)
+        for lt in range(mchan // 128):
+            mrows[lt, pl.ds(st * rows, 32 * rows), :] = flat[:, lt * 128:lt * 128 + 128]
+    for n in range(rows):
+        v = jnp.concatenate([mrows[lt, pl.ds(n, mtotal, stride=rows), :] for lt in range(mchan // 128)], axis=1)
+        mean = jnp.sum(v, axis=1, keepdims=True) * (1.0 / mchan)
+        d = v - mean
+        var = jnp.sum(d * d, axis=1, keepdims=True) * (1.0 / mchan)
+        y = (d * lax.rsqrt(var + LN_EPS) * mgam[...] + mbet[...]).astype(BF16)
+        acc = lax.dot_general(mw[...], y, (((1,), (1,)), ((), ())), preferred_element_type=F32)
+        bias = jnp.concatenate([mbias[...]] * (mtotal // 128), axis=1)
+        acc = ((acc + bias) * mmaskt[pl.ds(me * rows + n, 1), :]).astype(BF16)
+        am[pl.ds(n * hidden, hidden), :] = acc[:hidden]
+        gall[core, cy, cx, n // 2, pl.ds((n % 2) * hidden, hidden), :] = acc[hidden:]
+
+    def first_copy(part, d):
+        dy, dx = (0, d) if part == 0 else (d, 0)
+        here = gall.at[core, cy, cx, part]
+        k = part * 3 + d - 1
+        return pltpu.make_async_remote_copy(src_ref=here, dst_ref=here, send_sem=gs_sem.at[k], recv_sem=gr_sem.at[k],
+                                            device_id={'dap': device(dy, dx, 0)}, device_id_type=MESH_ID)
+
+    def second_copy(part, d):
+        dy, dx = (d, 0) if part == 0 else (0, d)
+        here = gall.at[core, cy, :, part] if part == 0 else gall.at[core, :, cx, part]
+        k = 6 + part * 3 + d - 1
+        return pltpu.make_async_remote_copy(src_ref=here, dst_ref=here, send_sem=gs_sem.at[k], recv_sem=gr_sem.at[k],
+                                            device_id={'dap': device(dy, dx, 0)}, device_id_type=MESH_ID)
+
+    def last_copy():
+        here = gall.at[core]
+        return pltpu.make_async_remote_copy(src_ref=here, dst_ref=here, send_sem=gs_sem.at[12], recv_sem=gr_sem.at[12],
+                                            device_id={'dap': device(0, 0, 1)}, device_id_type=MESH_ID)
+
+    for d in (1, 3, 2):
+        for part in range(2):
+            first_copy(part, d).start()
+    send(SEND_ORDER[4:8])
 
     mask_copy.wait()
     counts[...] = jnp.zeros_like(counts)
@@ -107,7 +132,49 @@
     lax.fori_loop(0, mraw.shape[0] // seqs, count_step, 0)
     maskt[...] = mraw[pl.ds(pl.multiple_of(me * seqs, seqs), seqs), :].astype(F32).T
 
+    for d in (1, 3, 2):
+        for part in range(2):
+            first_copy(part, d).wait()
+    for d in (1, 3, 2):
+        for part in range(2):
+            second_copy(part, d).start()
+    send(SEND_ORDER[8:])
+
     partner = device(0, 0, 1)
+    qn = 4
+    res = bown.shape[1]
+
+    def main_outer():
+        last_copy().wait()
+        tall = 2 * CORES * rows * hidden
+        r_id = lax.broadcasted_iota(jnp.int32, (tall, tall), 0)
+        c_id = lax.broadcasted_iota(jnp.int32, (tall, tall), 1)
+        target = ((r_id >> 2) & 1) * 256 + ((r_id >> 3) & 1) * 128 + (r_id & 3) * 32 + (r_id >> 4)
+        perm[...] = jnp.where(c_id == target, 1.0, 0.0).astype(BF16)
+
+        def perm_step(g, _):
+            gy, gx = g // 2, (g % 2) * 2
+            stack = jnp.concatenate([gall[cc, gy, pl.ds(gx, 2)].reshape(2 * rows * hidden, mtotal) for cc in range(CORES)], axis=0)
+            moved = jnp.dot(perm[...], stack, preferred_element_type=F32).reshape(hidden, 4 * rows, mtotal)
+            bm[:, pl.ds(pl.multiple_of(g * 4 * rows, 4 * rows), 4 * rows), :] = moved.astype(BF16)
+            return 0
+
+        lax.fori_loop(0, 8, perm_step, 0)
+
+        def q_step(qt, _):
+            rhs = bm[pl.ds(qt * qn, qn)].reshape(qn * res, mtotal)
+            prod = lax.dot_general(am[...], rhs, (((1,), (1,)), ((), ())), preferred_element_type=F32).astype(BF16)
+            for i in range(rows):
+                for q in range(qn):
+                    osc[i, pl.ds(pl.multiple_of(qt * (qn * hidden) + q * hidden, hidden), hidden), :] = prod[i * hidden:(i + 1) * hidden, q * res:(q + 1) * res]
+            return 0
+
+        lax.fori_loop(0, hidden // qn, q_step, 0)
+        for r in range(0, rows, 2):
+            pair = jnp.dot(mwt[...], jnp.concatenate([osc[r], osc[r + 1]], axis=1), preferred_element_type=F32)
+            rmain[r] = pair[:, :res]
+            rmain[r + 1] = pair[:, res:]
+
     chip_rows = rows * CORES
     pair_rows = 2 * chip_rows
 
@@ -137,6 +204,17 @@
                 pltpu.make_async_remote_copy(src_ref=xb.at[own], dst_ref=xb.at[own], send_sem=xs_sem.at[k], recv_sem=xr_sem.at[k],
                                              device_id={'dap': partner}, device_id_type=MESH_ID).wait_recv()
         xout_copy(u).start()
+
+        @pl.when(pos == 2)
+        def _():
+            for d in (1, 3, 2):
+                for part in range(2):
+                    second_copy(part, d).wait()
+            last_copy().start()
+
+        @pl.when(pos == 4)
+        def _():
+            main_outer()
 
         def norm_step(n, _):
             for lt in range(seqs // 128):
@@ -184,9 +262,6 @@
 
     lax.fori_loop(0, 8, exch_wait, 0)
 
-    qn = 4
-    res = bown.shape[1]
-
     def block_step(b, _):
         half = (cx // 2 + 1 - b % 2) % 2
         dys = (1 + b // 2, 3 - 3 * (b // 2))
@@ -231,21 +306,28 @@
     for r in range(rows):
         acc = lax.fori_loop(1, SIDE * SIDE, lambda s, a: a + rrecv[s, r].astype(F32), rsend[chip, r].astype(F32))
         term = (acc + bo[...]) / (NORM_EPS + counts[pl.ds(me * rows + r, 1), :])
-        out_ref[r] = z_ref[r] + term.T
+        mterm = (rmain[r] + mbo[...]) / (NORM_EPS + mcounts[pl.ds(me * rows + r, 1), :])
+        out_ref[r] = (z_ref[r] + term.T) + mterm.T
 
     def x_wait(k, _):
         pltpu.make_async_remote_copy(src_ref=x_hbm.at[:, :, cols(me)], dst_ref=xb.at[own], send_sem=xs_sem.at[k], recv_sem=xr_sem.at[k],
                                      device_id={'dap': partner}, device_id_type=MESH_ID).wait_send()
+        pltpu.make_async_remote_copy(src_ref=main_hbm.at[pl.ds(0, mseqs)], dst_ref=mout_hbm.at[:, me], send_sem=cs_sem.at[k], recv_sem=cr_sem.at[k],
+                                     device_id={'dap': partner}, device_id_type=MESH_ID).wait()
         return 0
 
     lax.fori_loop(1, SIDE * SIDE * CORES, x_wait, 0)
-
-
-def extra_call(x, mask, z, ln_gamma, ln_beta, w_left, b_left, w_right, b_right, w_out, b_out):
+    pltpu.make_async_copy(main_hbm.at[pl.ds(me * mseqs, mseqs)], mout_hbm.at[:, me], cr_sem.at[0]).wait()
+
+
+def opm_call(x, mask, z, main, mmask, extra_weights, main_weights):
     rows, chan, total = x.shape
     devices = SIDE * SIDE * CORES
     res = rows * devices
     seqs = total // devices
+    ln_gamma, ln_beta, w_left, b_left, w_right, b_right, w_out, b_out = extra_weights
+    m_gamma, m_beta, mw_left, mb_left, mw_right, mb_right, mw_out, mb_out = main_weights
+    mtotal, _, mchan = main.shape
     hidden = w_left.shape[1]
     width = w_out.shape[1]
     chip_rows = rows * CORES
@@ -256,37 +338,51 @@
     lanes = lambda v: jnp.broadcast_to(v.astype(F32)[:, None], (v.shape[0], 128))
     gam, bet, ba = lanes(ln_gamma), lanes(ln_beta), lanes(b_left)
     bb = lanes(jnp.repeat(b_right, chip_rows))
-    bo = lanes(b_out)
-    wt = w_out.reshape(hidden, hidden, width).transpose(2, 1, 0).reshape(width, hidden * hidden)
+    bo, mbo = lanes(b_out), lanes(mb_out)
+    turn = lambda w: w.reshape(hidden, hidden, width).transpose(2, 1, 0).reshape(width, hidden * hidden)
+    wt, mwt = turn(w_out), turn(mw_out)
+    mw = jnp.concatenate([mw_left, mw_right], axis=1).T
+    mbias = lanes(jnp.concatenate([mb_left, mb_right]))
+    mgam, mbet = m_gamma.astype(F32)[None], m_beta.astype(F32)[None]
     vm = pl.BlockSpec(memory_space=pltpu.VMEM)
     hb = pl.BlockSpec(memory_space=pl.ANY)
     dma = pltpu.SemaphoreType.DMA
-    flops = 2 * (total // 16) * (res // 2) * hidden * res * hidden
+    chips = SIDE * SIDE
+    flops = 2 * (total // chips) * (res // 2) * hidden * res * hidden
     return pl.pallas_call(
-        extra_kernel,
-        out_shape=(jax.ShapeDtypeStruct((res, chan, seqs), BF16), jax.ShapeDtypeStruct(z.shape, F32)),
-        in_specs=[hb, hb] + [vm] * 9,
-        out_specs=(hb, vm),
+        opm_kernel,
+        out_shape=(jax.ShapeDtypeStruct((res, chan, seqs), BF16), jax.ShapeDtypeStruct(z.shape, F32), jax.ShapeDtypeStruct((mtotal // devices, devices, rows, mchan), BF16)),
+        in_specs=[hb, hb, hb] + [vm] * 17,
+        out_specs=(hb, vm, hb),
         scratch_shapes=[
             pltpu.VMEM((res, chan, seqs), BF16),
             pltpu.VMEM((2 * chip_rows * chan, seqs), BF16),
-            pltpu.VMEM((16, rows * hidden, seqs), BF16),
-            pltpu.VMEM((16, rows * hidden, seqs), BF16),
+            pltpu.VMEM((chips, rows * hidden, seqs), BF16),
+            pltpu.VMEM((chips, rows * hidden, seqs), BF16),
             pltpu.VMEM((hidden, res, seqs), BF16),
             pltpu.VMEM((hidden, res, seqs), BF16),
-            pltpu.VMEM((16, rows * hidden, seqs), BF16),
+            pltpu.VMEM((chips, rows * hidden, seqs), BF16),
             pltpu.VMEM((4 * rows, hidden * hidden, res), BF16),
-            pltpu.VMEM((16, rows, width, res), BF16),
-            pltpu.VMEM((16, rows, width, res), BF16),
+            pltpu.VMEM((chips, rows, width, res), BF16),
+            pltpu.VMEM((chips, rows, width, res), BF16),
             pltpu.VMEM((total, res), jnp.int32),
             pltpu.VMEM((res, seqs), F32),
             pltpu.VMEM((res, res), F32),
-            dma((devices,)), dma((devices,)), dma((8,)), dma, dma((8,)), dma((8,)), dma((8,)), dma((8,)), dma((16,)), dma((16,)),
+            pltpu.VMEM((mchan // 128, mtotal * rows, 128), F32),
+            pltpu.VMEM((rows * hidden, mtotal), BF16),
+            pltpu.VMEM((2 * chip_rows * hidden, 2 * chip_rows * hidden), BF16),
+            pltpu.VMEM((CORES, SIDE, SIDE, 2, rows // 2 * hidden, mtotal), BF16),
+            pltpu.VMEM((hidden, res, mtotal), BF16),
+            pltpu.VMEM((rows, width, res), F32),
+            pltpu.VMEM((res, mtotal), F32),
+            pltpu.VMEM((res, res), F32),
+            dma((devices,)), dma((devices,)), dma((8,)), dma, dma((8,)), dma((8,)), dma((8,)), dma((8,)), dma((chips,)), dma((chips,)),
+            dma((devices,)), dma((devices,)), dma((13,)), dma((13,)),
         ],
         compiler_params=pltpu.CompilerParams(collective_id=0, has_side_effects=True, vmem_limit_bytes=60 * 1024 * 1024),
         cost_estimate=pl.CostEstimate(flops=flops, bytes_accessed=20_000_000, transcendentals=0),
-        name='extra_opm',
-    )(x, mask, z, akron, bkron, gam, bet, ba, bb, wt, bo)
+        name='opm',
+    )(x, mask, main, z, akron, bkron, gam, bet, ba, bb, wt, bo, main, mmask, mgam, mbet, mw, mbias, mwt, mbo)
 
 
 def solution(mesh):
@@ -294,12 +390,10 @@
     mask_spec = P('data', None)
     row_spec = P(('data', 'dap'), None, None)
 
-    def local_program(extra_block, extra_mask, main_block, main_mask, pair_rows, extra_ln_gamma, extra_ln_beta, extra_w_left, extra_b_left, extra_w_right, extra_b_right, extra_w_out, extra_b_out, main_ln_gamma, main_ln_beta, main_w_left, main_b_left, main_w_right, main_b_right, main_w_out, main_b_out):
-        relaid, summed = extra_call(extra_block.transpose(1, 2, 0), extra_mask, pair_rows, extra_ln_gamma, extra_ln_beta, extra_w_left, extra_b_left, extra_w_right, extra_b_right, extra_w_out, extra_b_out)
-        extra_relaid = relaid.transpose(2, 0, 1)
-        main_term = gathered_term(main_block, main_mask, main_ln_gamma, main_ln_beta, main_w_left, main_b_left, main_w_right, main_b_right, main_w_out, main_b_out)
-        main_relaid = lax.all_to_all(main_block, 'dap', 0, 1, tiled=True)
-        return summed + main_term, extra_relaid, main_relaid
+    def local_program(extra_block, extra_mask, main_block, main_mask, pair_rows, *weights):
+        relaid, pair_out, main_relaid = opm_call(extra_block.transpose(1, 2, 0), extra_mask, pair_rows, main_block, main_mask, weights[:8], weights[8:])
+        mseqs, _, _, mchan = main_relaid.shape
+        return pair_out, relaid.transpose(2, 0, 1), main_relaid.reshape(mseqs, -1, mchan)
 
     in_specs = (value_a8, mask_spec, value_a8, mask_spec, row_spec) + (P(),) * 16
     return jax.shard_map(local_program, mesh=mesh, in_specs=in_specs, out_specs=(row_spec, row_spec, row_spec), check_vma=False)

time: 194 us -> 179 us (0.923)
  Pallas kernels: 128 us -> 144 us
  between operations: 14.3 us -> 0.68 us
  starting transfers between devices: 8.24 us -> 0 us
  matrix products: 7.13 us -> 0 us
    pallas_call x1, Pallas kernels: 128 us -> 144 us  [opm_call(): pl.pallas_call(opm_kernel, out_shape=(jax.ShapeDtypeStruct((res, chan, se...]
    all_to_all x1 -> x0, starting transfers between devices: 8.18 us -> none  [local_program(): main_relaid = lax.all_to_all(main_block, 'dap', 0, 1, tiled=True)]
    dot_general x4 -> x0, matrix products: 7.13 us -> none  [the longest x1 4.8 us: gathered_term(): jnp.einsum('sic,sjd->ijcd', left_proj, right_all, preferred_element_type=...]
    convert_element_type x2 -> x1, local copies, waits for them, and re-layouts: 7.06 us -> 0.09 us  [opm_call(): v.astype(F32)[:, None]]
    broadcast_in_dim x6 -> x8, local copies, waits for them, and re-layouts: 3.59 us -> 8.9 us  [the longest x7 8.17 us: opm_call(): jnp.broadcast_to(v.astype(F32)[:, None], (v.shape[0], 128))]
    reduce_sum x2 -> x0, other arithmetic: 3.18 us -> none  [the longest x1 1.75 us: layer_norm(): row_var = jnp.mean(centered * centered, axis=-1, keepdims=True)]
    convert_element_type x8 -> x3, other arithmetic: 3.75 us -> 0.76 us  [the longest x1 0.75 us: opm_call(): v.astype(F32)[:, None]]
    broadcast_in_dim x0 -> x2, other arithmetic: none -> 2.46 us  [opm_call(): mgam, mbet = (m_gamma.astype(F32)[None], m_beta.astype(F32)[None])]
  transfers between devices with their start and end apart: 2 -> 0, of which waited for: 0 -> 0; matrix products, arithmetic and copies ran while one was open for 9% -> 0% of each run, Pallas kernels for 67% -> 0%
where the time goes in v2:
time: 179 us; the launch traced here: 177 us
  Pallas kernels  144 us (80%)
  local copies, waits for them, and re-layouts  25.8 us (14%)
  other arithmetic  6.19 us (3%)
    pallas_call x1, Pallas kernels, opm_call(): pl.pallas_call(opm_kernel, out_shape=(jax.ShapeDtypeStruct((res, chan, se...  144 us
    unnamed x6, local copies, waits for them, and re-layouts  10.3 us
    broadcast_in_dim x7, local copies, waits for them, and re-layouts, opm_call(): jnp.broadcast_to(v.astype(F32)[:, None], (v.shape[0], 128))  8.17 us

profile of v2, /device:TPU:98, one launch (start us, length us, event | category | flops | bytes accessed | tf_op | source)
XLA Modules:
  0.0 177.0 jit_solution(3799467489123724780)
XLA Ops:
  0.6 0.7 maximum_convert_fusion
  1.4 1.2 broadcast_in_dim.71
  2.6 1.2 broadcast_in_dim.72
  3.9 1.3 broadcast_in_dim.26.ba
  5.2 0.7 broadcast_in_dim.27
  5.9 0.1 convert_element_type.55
  6.0 0.7 broadcast_in_dim.34.mbias
  6.7 1.3 broadcast_in_dim.24.gam
  8.0 1.3 broadcast_in_dim.25.bet
  9.4 1.4 maximum_bitcast_fusion.mw
  10.7 1.4 broadcast_in_dim.29.bo
  12.1 1.4 broadcast_in_dim.70.mbo
  13.4 0.7 broadcast_in_dim.28.bb
  14.2 0.8 broadcast_multiply_fusion.1
  15.0 0.8 mul.37.akron
  15.8 1.1 copy.30
  16.8 0.9 copy.32.wt
  17.7 1.1 copy.31
  18.7 0.9 copy.33.mwt
  19.6 0.8 broadcast_multiply_fusion
  20.4 1.0 mul.41.bkron
  21.4 144.2 %opm.1 = (bf16[128,64,384]{2,1,0:T(8,128)(2,1)}, f32[4,128,128]{2,1,0:T(8,128)}, bf16[8,32,4,256]{3,2,1,0:T(4,128)(2,1)}) custom-call(bf16[4,64,12288]{2,1,0:T(8,128)(2,1)} %bitcast.25, s32[12288,128]{1,0:T(8,128)} %mask_hbm.1, bf16[256,4,256]{2,1,0:T(4,128)(2,1)} %main_ref.1, f32[4,128,128]{2,1,0:T(8,128)} %z_ref.1, bf16[128,256]{1,0:T(8,128)(2,1)} %mul.37.akron, ...), custom_call_target="tpu_custom_call" | custom-call | flops 12884901888 | bytes 20000000 | tf_op jit(solution)/shard_map/opm/pallas_call | solution.py:352
  165.7 0.0 copy-start
  165.7 0.0 copy-start.1
  165.7 9.6 %copy.34 = bf16[384,128,64]{1,2,0:T(8,128)(2,1)} copy(bf16[384,128,64]{0,2,1:T(8,128)(2,1)} %bitcast.18) | data formatting | bytes 12582912
  175.3 0.0 copy-done
  175.3 0.9 reshape.78
  176.3 0.0 copy-done.1
  176.3 0.7 copy.36
  (2 shorter events, 0.0 us)
Async XLA Ops:
  165.7 9.7 %copy-start = (bf16[8,32,4,256]{3,2,1,0:T(4,128)(2,1)S(1)}, bf16[8,32,4,256]{3,2,1,0:T(4,128)(2,1)}, u32[]{:S(2)}) copy-start(bf16[8,32,4,256]{3,2,1,0:T(4,128)(2,1)} %get-tuple-element.8) | copy-start | bytes 1572868
  165.7 10.6 %copy-start.1 = (f32[4,128,128]{2,1,0:T(8,128)S(1)}, f32[4,128,128]{2,1,0:T(8,128)}, u32[]{:S(2)}) copy-start(f32[4,128,128]{2,1,0:T(8,128)} %get-tuple-element.21) | copy-start | bytes 786436

commit v3 on v2

--- a/solution.py
+++ b/solution.py
@@ -17,10 +17,16 @@
 SEND_ORDER = ((1, 1), (3, 3), (1, 3), (3, 1), (1, 2), (3, 2), (1, 0), (3, 0), (2, 2), (0, 2), (2, 1), (2, 3), (0, 1), (2, 0), (0, 3))
 
 
-def opm_kernel(x_hbm, mask_hbm, main_hbm, z_ref, akron, bkron, gam, bet, ba, bb, wt, bo,
-               main_ref, mmask, mgam, mbet, mw, mbias, mwt, mbo,
+def spread(ref):
+    v = ref[...].astype(F32)
+    return jnp.broadcast_to(v.reshape(1, v.shape[0]), (128, v.shape[0])).T
+
+
+def opm_kernel(x_hbm, mask_hbm, main_hbm, z_ref, g_in, be_in, wl_in, bl_in, wr_in, br_in, wo_in, bo_in,
+               main_ref, mmask, mg_in, mbe_in, mwl_in, mbl_in, mwr_in, mbr_in, mwo_in, mbo_in,
                xout_hbm, out_ref, mout_hbm,
                xb, xn, aown, apart, bown, bpart, astage, osc, rsend, rrecv, mraw, maskt, counts,
+               akron, bkron, gam, bet, ba, bb, wt, bo, mgam, mbet, mw, mbias, mwt, mbo, wrows,
                mrows, am, perm, gall, bm, rmain, mmaskt, mcounts,
                xs_sem, xr_sem, xo_sem, ms_sem, as_sem, ar_sem, bs_sem, br_sem, rs_sem, rr_sem,
                cs_sem, cr_sem, gs_sem, gr_sem):
@@ -78,9 +84,15 @@
     pltpu.make_async_copy(main_hbm.at[pl.ds(me * mseqs, mseqs)], mout_hbm.at[:, me], cr_sem.at[0]).start()
     send(SEND_ORDER[:4])
 
+    mchan = main_ref.shape[2]
+    mgam[...] = mg_in[...].astype(F32).reshape(1, mchan)
+    mbet[...] = mbe_in[...].astype(F32).reshape(1, mchan)
+    for k, (w, bv) in enumerate(((mwl_in, mbl_in), (mwr_in, mbr_in))):
+        mw[pl.ds(k * hidden, hidden), :] = w[...]
+        mbias[pl.ds(k * hidden, hidden), :] = spread(bv)
+
     mmaskt[...] = mmask[...].astype(F32).T
     mcounts[...] = jnp.dot(mmaskt[...].astype(BF16), mmask[...].astype(F32).astype(BF16), preferred_element_type=F32)
-    mchan = main_ref.shape[2]
     for st in range(0, mtotal, 32):
         flat = main_ref[pl.ds(st, 32)].astype(F32).reshape(32 * rows, mchan)
         for lt in range(mchan // 128):
@@ -120,6 +132,34 @@
         for part in range(2):
             first_copy(part, d).start()
     send(SEND_ORDER[4:8])
+
+    gam[...] = spread(g_in)
+    bet[...] = spread(be_in)
+    ba[...] = spread(bl_in)
+    bo[...] = spread(bo_in)
+    mbo[...] = spread(mbo_in)
+    for w, dst in ((wo_in, wt), (mwo_in, mwt)):
+        wrows[...] = w[...].astype(F32)
+        for q0 in range(0, hidden, 8):
+            rows_q = jnp.concatenate([wrows[pl.ds(q, hidden, stride=hidden), :] for q in range(q0, q0 + 8)], axis=0)
+            dst[:, pl.ds(q0 * hidden, 8 * hidden)] = rows_q.T.astype(BF16)
+    left = wl_in[...].astype(F32)
+    left = jnp.concatenate([left, left], axis=1)
+    left = jnp.concatenate([left] * (rows * chan // 128), axis=1)
+    lane = lax.broadcasted_iota(jnp.int32, left.shape, 1)
+    for r in range(rows):
+        akron[pl.ds(r * hidden, hidden), :] = jnp.where((lane >= r * chan) & (lane < (r + 1) * chan), left, 0.0).astype(BF16)
+    group = rows * CORES
+    right = wr_in[...].astype(F32)
+    right = jnp.concatenate([right, right], axis=1)
+    right = jnp.broadcast_to(right[:, None, :], (hidden, group, 128)).reshape(hidden * group, 128)
+    row = lax.broadcasted_iota(jnp.int32, right.shape, 0) & (group - 1)
+    lane = lax.broadcasted_iota(jnp.int32, right.shape, 1)
+    for lt in range(group * chan // 128):
+        first = lt * (128 // chan)
+        keep = ((row == first) & (lane < chan)) | ((row == first + 1) & (lane >= chan))
+        bkron[:, pl.ds(lt * 128, 128)] = jnp.where(keep, right, 0.0).astype(BF16)
+    bb[...] = jnp.broadcast_to(spread(br_in)[:, None, :], (hidden, group, 128)).reshape(hidden * group, 128)
 
     mask_copy.wait()
     counts[...] = jnp.zeros_like(counts)
@@ -331,19 +371,6 @@
     hidden = w_left.shape[1]
     width = w_out.shape[1]
     chip_rows = rows * CORES
-    eye_a = jnp.eye(rows, dtype=BF16)
-    eye_b = jnp.eye(chip_rows, dtype=BF16)
-    akron = (eye_a[:, None, :, None] * w_left.T[None, :, None, :]).reshape(rows * hidden, rows * chan)
-    bkron = (w_right.T[:, None, None, :] * eye_b[None, :, :, None]).reshape(hidden * chip_rows, chip_rows * chan)
-    lanes = lambda v: jnp.broadcast_to(v.astype(F32)[:, None], (v.shape[0], 128))
-    gam, bet, ba = lanes(ln_gamma), lanes(ln_beta), lanes(b_left)
-    bb = lanes(jnp.repeat(b_right, chip_rows))
-    bo, mbo = lanes(b_out), lanes(mb_out)
-    turn = lambda w: w.reshape(hidden, hidden, width).transpose(2, 1, 0).reshape(width, hidden * hidden)
-    wt, mwt = turn(w_out), turn(mw_out)
-    mw = jnp.concatenate([mw_left, mw_right], axis=1).T
-    mbias = lanes(jnp.concatenate([mb_left, mb_right]))
-    mgam, mbet = m_gamma.astype(F32)[None], m_beta.astype(F32)[None]
     vm = pl.BlockSpec(memory_space=pltpu.VMEM)
     hb = pl.BlockSpec(memory_space=pl.ANY)
     dma = pltpu.SemaphoreType.DMA
@@ -352,7 +379,7 @@
     return pl.pallas_call(
         opm_kernel,
         out_shape=(jax.ShapeDtypeStruct((res, chan, seqs), BF16), jax.ShapeDtypeStruct(z.shape, F32), jax.ShapeDtypeStruct((mtotal // devices, devices, rows, mchan), BF16)),
-        in_specs=[hb, hb, hb] + [vm] * 17,
+        in_specs=[hb, hb, hb] + [vm] * 19,
         out_specs=(hb, vm, hb),
         scratch_shapes=[
             pltpu.VMEM((res, chan, seqs), BF16),
@@ -368,6 +395,21 @@
             pltpu.VMEM((total, res), jnp.int32),
             pltpu.VMEM((res, seqs), F32),
             pltpu.VMEM((res, res), F32),
+            pltpu.VMEM((rows * hidden, rows * chan), BF16),
+            pltpu.VMEM((hidden * chip_rows, chip_rows * chan), BF16),
+            pltpu.VMEM((chan, 128), F32),
+            pltpu.VMEM((chan, 128), F32),
+            pltpu.VMEM((hidden, 128), F32),
+            pltpu.VMEM((hidden * chip_rows, 128), F32),
+            pltpu.VMEM((width, hidden * hidden), BF16),
+            pltpu.VMEM((width, 128), F32),
+            pltpu.VMEM((1, mchan), F32),
+            pltpu.VMEM((1, mchan), F32),
+            pltpu.VMEM((2 * hidden, mchan), BF16),
+            pltpu.VMEM((2 * hidden, 128), F32),
+            pltpu.VMEM((width, hidden * hidden), BF16),
+            pltpu.VMEM((width, 128), F32),
+            pltpu.VMEM((hidden * hidden, width), F32),
             pltpu.VMEM((mchan // 128, mtotal * rows, 128), F32),
             pltpu.VMEM((rows * hidden, mtotal), BF16),
             pltpu.VMEM((2 * chip_rows * hidden, 2 * chip_rows * hidden), BF16),
@@ -382,7 +424,8 @@
         compiler_params=pltpu.CompilerParams(collective_id=0, has_side_effects=True, vmem_limit_bytes=60 * 1024 * 1024),
         cost_estimate=pl.CostEstimate(flops=flops, bytes_accessed=20_000_000, transcendentals=0),
         name='opm',
-    )(x, mask, main, z, akron, bkron, gam, bet, ba, bb, wt, bo, main, mmask, mgam, mbet, mw, mbias, mwt, mbo)
+    )(x, mask, main, z, ln_gamma, ln_beta, w_left.T, b_left, w_right.T, b_right, w_out, b_out,
+      main, mmask, m_gamma, m_beta, mw_left.T, mb_left, mw_right.T, mb_right, mw_out, mb_out)
 
 
 def solution(mesh):

time: 179 us -> 158 us (0.88)
  local copies, waits for them, and re-layouts: 25.8 us -> 11.3 us
  other arithmetic: 6.19 us -> 0 us
    broadcast_in_dim x8 -> x0, local copies, waits for them, and re-layouts: 8.9 us -> none  [the longest x7 8.17 us: opm_call(): jnp.broadcast_to(v.astype(F32)[:, None], (v.shape[0], 128))]
    broadcast_in_dim x2 -> x0, other arithmetic: 2.46 us -> none  [opm_call(): mgam, mbet = (m_gamma.astype(F32)[None], m_beta.astype(F32)[None])]
    transpose x2 -> x0, local copies, waits for them, and re-layouts: 2.11 us -> none  [opm_call(): w.reshape(hidden, hidden, width).transpose(2, 1, 0)]
    mul x2 -> x0, local copies, waits for them, and re-layouts: 1.8 us -> none  [the longest x1 1.03 us: opm_call(): w_right.T[:, None, None, :] * eye_b[None, :, :, None]]
where the time goes in v3:
time: 158 us; the launch traced here: 156 us
  Pallas kernels  144 us (91%)
  local copies, waits for them, and re-layouts  11.3 us (7%)
    pallas_call x1, Pallas kernels, opm_call(): pl.pallas_call(opm_kernel, out_shape=(jax.ShapeDtypeStruct((res, chan, se...  144 us
    unnamed x6, local copies, waits for them, and re-layouts  10.3 us

profile of v3, /device:TPU:98, one launch (start us, length us, event | category | flops | bytes accessed | tf_op | source)
XLA Modules:
  0.0 156.2 jit_solution(1739788614153849005)
XLA Ops:
  0.6 144.2 %opm.1 = (bf16[128,64,384]{2,1,0:T(8,128)(2,1)}, f32[4,128,128]{2,1,0:T(8,128)}, bf16[8,32,4,256]{3,2,1,0:T(4,128)(2,1)}) custom-call(bf16[4,64,12288]{2,1,0:T(8,128)(2,1)} %bitcast.7, s32[12288,128]{1,0:T(8,128)} %mask_hbm.1, bf16[256,4,256]{2,1,0:T(4,128)(2,1)} %main_ref.1, f32[4,128,128]{2,1,0:T(8,128)} %z_ref.1, bf16[64]{0:T(256)(128)(2,1)} %g_in.1, ...), custom_call_target="tpu_custom_call" | custom-call | flops 12884901888 | bytes 20000000 | tf_op jit(solution)/shard_map/opm/pallas_call | solution.py:379
  144.9 0.0 copy-start
  144.9 0.0 copy-start.1
  144.9 9.6 %copy.24 = bf16[384,128,64]{1,2,0:T(8,128)(2,1)} copy(bf16[384,128,64]{0,2,1:T(8,128)(2,1)} %bitcast.6) | data formatting | bytes 12582912
  154.5 0.0 copy-done
  154.5 0.9 reshape.9
  155.4 0.0 copy-done.1
  155.4 0.7 copy.26
Async XLA Ops:
  144.9 9.7 %copy-start = (bf16[8,32,4,256]{3,2,1,0:T(4,128)(2,1)S(1)}, bf16[8,32,4,256]{3,2,1,0:T(4,128)(2,1)}, u32[]{:S(2)}) copy-start(bf16[8,32,4,256]{3,2,1,0:T(4,128)(2,1)} %get-tuple-element.8) | copy-start | bytes 1572868
  144.9 10.6 %copy-start.1 = (f32[4,128,128]{2,1,0:T(8,128)S(1)}, f32[4,128,128]{2,1,0:T(8,128)}, u32[]{:S(2)}) copy-start(f32[4,128,128]{2,1,0:T(8,128)} %get-tuple-element.15) | copy-start | bytes 786436

commit v4 on v3

--- a/solution.py
+++ b/solution.py
@@ -14,7 +14,9 @@
 MESH_ID = pl.DeviceIdType.MESH
 SIDE = 4
 CORES = 2
-SEND_ORDER = ((1, 1), (3, 3), (1, 3), (3, 1), (1, 2), (3, 2), (1, 0), (3, 0), (2, 2), (0, 2), (2, 1), (2, 3), (0, 1), (2, 0), (0, 3))
+SEND_ORDER = ((1, 1), (3, 3), (1, 3), (3, 1), (2, 2), (2, 1), (0, 2), (2, 3), (0, 1), (0, 3), (1, 2), (2, 0), (3, 2), (1, 0), (3, 0))
+ROW_ORDER = (2, 1, 3, 0)
+PAIR_ORDER = ((2, 1), (0, 1), (0, 0), (1, 1), (2, 0), (3, 1), (1, 0), (3, 0))
 
 
 def spread(ref):
@@ -25,11 +27,11 @@
 def opm_kernel(x_hbm, mask_hbm, main_hbm, z_ref, g_in, be_in, wl_in, bl_in, wr_in, br_in, wo_in, bo_in,
                main_ref, mmask, mg_in, mbe_in, mwl_in, mbl_in, mwr_in, mbr_in, mwo_in, mbo_in,
                xout_hbm, out_ref, mout_hbm,
-               xb, xn, aown, apart, bown, bpart, astage, osc, rsend, rrecv, mraw, maskt, counts,
+               xb, xn, aown, apart, bown, bpart, astage, osc, rsend, ra, rb, pasend, pa, pbsend, pb, mraw, maskt, counts,
                akron, bkron, gam, bet, ba, bb, wt, bo, mgam, mbet, mw, mbias, mwt, mbo, wrows,
                mrows, am, perm, gall, bm, rmain, mmaskt, mcounts,
-               xs_sem, xr_sem, xo_sem, ms_sem, as_sem, ar_sem, bs_sem, br_sem, rs_sem, rr_sem,
-               cs_sem, cr_sem, gs_sem, gr_sem):
+               xs_sem, xr_sem, xo_sem, ms_sem, as_sem, ar_sem, bs_sem, br_sem,
+               cs_sem, cr_sem, gs_sem, gr_sem, ras_sem, rar_sem, rbs_sem, rbr_sem, pas_sem, par_sem, pbs_sem, pbr_sem):
     me = lax.axis_index('dap')
     core = me % CORES
     chip = me // CORES
@@ -77,10 +79,8 @@
         for dy, dx in order:
             for dc in range(CORES):
                 x_copy(dy, dx, dc).start()
-                main_copy(dy, dx, dc).start()
 
     x_copy(0, 0, 1).start()
-    main_copy(0, 0, 1).start()
     pltpu.make_async_copy(main_hbm.at[pl.ds(me * mseqs, mseqs)], mout_hbm.at[:, me], cr_sem.at[0]).start()
     send(SEND_ORDER[:4])
 
@@ -181,7 +181,7 @@
     send(SEND_ORDER[8:])
 
     partner = device(0, 0, 1)
-    qn = 4
+    qn = 8
     res = bown.shape[1]
 
     def main_outer():
@@ -232,9 +232,8 @@
         return pltpu.make_async_copy(xb.at[at], xout_hbm.at[at], xo_sem.at[u])
 
     def unit_step(pos, _):
-        late = pos // 4
-        dy = (1 - late) * (1 + 2 * (pos % 2)) + late * (2 - 2 * (pos % 2))
-        half = (cx // 2 + 1 - (pos // 2) % 2) % 2
+        dy = sum((pos == k).astype(jnp.int32) * v for k, (v, _) in enumerate(PAIR_ORDER) if v)
+        half = (cx // 2 + sum((pos == k).astype(jnp.int32) for k, (_, v) in enumerate(PAIR_ORDER) if v)) % 2
         ysrc = (cy - dy + SIDE) % SIDE
         u = ysrc * 2 + half
         for xx in range(2):
@@ -294,6 +293,11 @@
 
     lax.fori_loop(0, 8, unit_step, 0)
 
+    main_copy(0, 0, 1).start()
+    for dy, dx in SEND_ORDER:
+        for dc in range(CORES):
+            main_copy(dy, dx, dc).start()
+
     def exch_wait(u, _):
         a_copy(u).wait()
         b_copy(u).wait()
@@ -302,52 +306,107 @@
 
     lax.fori_loop(0, 8, exch_wait, 0)
 
+    def ra_copy(dy, dx):
+        row = (cy + dy) % SIDE
+        k = dy * (SIDE - 1) + dx - 1
+        return pltpu.make_async_remote_copy(src_ref=rsend.at[row, (cx + dx) % SIDE, pl.ds(0, 2)], dst_ref=ra.at[row, dx - 1], send_sem=ras_sem.at[k], recv_sem=rar_sem.at[k],
+                                            device_id={'dap': device(0, dx, 0)}, device_id_type=MESH_ID)
+
+    def rb_copy(dy):
+        return pltpu.make_async_remote_copy(src_ref=rsend.at[(cy + dy) % SIDE, :, pl.ds(2, 2)], dst_ref=rb.at[dy - 1], send_sem=rbs_sem.at[dy - 1], recv_sem=rbr_sem.at[dy - 1],
+                                            device_id={'dap': device(dy, 0, 0)}, device_id_type=MESH_ID)
+
+    def pa_copy(dy):
+        return pltpu.make_async_remote_copy(src_ref=pasend.at[dy - 1], dst_ref=pa.at[dy - 1], send_sem=pas_sem.at[dy - 1], recv_sem=par_sem.at[dy - 1],
+                                            device_id={'dap': device(dy, 0, 0)}, device_id_type=MESH_ID)
+
+    def pb_copy(dx):
+        return pltpu.make_async_remote_copy(src_ref=pbsend.at[dx - 1], dst_ref=pb.at[dx - 1], send_sem=pbs_sem.at[dx - 1], recv_sem=pbr_sem.at[dx - 1],
+                                            device_id={'dap': device(0, dx, 0)}, device_id_type=MESH_ID)
+
+    def row_offset(b):
+        return sum((b == k).astype(jnp.int32) * v for k, v in enumerate(ROW_ORDER) if v)
+
     def block_step(b, _):
-        half = (cx // 2 + 1 - b % 2) % 2
-        dys = (1 + b // 2, 3 - 3 * (b // 2))
-        starts = [((cy + dy) % SIDE) * SIDE + 2 * half for dy in dys]
+        dy = row_offset(b)
+        row = (cy + dy) % SIDE
+        tall = SIDE * rows * hidden
 
         def q_step(qt, _):
-            lhs = jnp.concatenate([jnp.concatenate([ref[pl.ds(t, 2)].reshape(2 * rows * hidden, seqs) for t in starts], axis=0) for ref in (aown, apart)], axis=1)
+            lhs = jnp.concatenate([ref[pl.ds(row * SIDE, SIDE)].reshape(tall, seqs) for ref in (aown, apart)], axis=1)
             rhs = jnp.concatenate([ref[pl.ds(qt * qn, qn)].reshape(qn * res, seqs) for ref in (bown, bpart)], axis=1)
             prod = lax.dot_general(lhs, rhs, (((1,), (1,)), ((), ())), preferred_element_type=F32).astype(BF16)
-            for i in range(4 * rows):
+            for i in range(SIDE * rows):
                 for q in range(qn):
                     osc[i, pl.ds(pl.multiple_of(qt * (qn * hidden) + q * hidden, hidden), hidden), :] = prod[i * hidden:(i + 1) * hidden, q * res:(q + 1) * res]
             return 0
 
         lax.fori_loop(0, hidden // qn, q_step, 0)
-        for c4 in range(4):
-            t = starts[c4 // 2] + c4 % 2
+        for t in range(SIDE):
             for r in range(0, rows, 2):
-                i = c4 * rows + r
+                i = t * rows + r
                 rhs = jnp.concatenate([osc[i], osc[i + 1]], axis=1)
                 pair = jnp.dot(wt[...], rhs, preferred_element_type=F32).astype(BF16)
-                rsend[t, r] = pair[:, :res]
-                rsend[t, r + 1] = pair[:, res:]
-            dy = dys[c4 // 2]
-            dx = (t % SIDE - cx + SIDE) % SIDE
-            slot = dy * SIDE + dx
-
-            @pl.when(slot != 0)
-            def _():
-                pltpu.make_async_remote_copy(src_ref=rsend.at[t], dst_ref=rrecv.at[slot], send_sem=rs_sem.at[slot], recv_sem=rr_sem.at[slot],
-                                             device_id={'dap': t * CORES + core}, device_id_type=MESH_ID).start()
+                rsend[row, t, r] = pair[:, :res]
+                rsend[row, t, r + 1] = pair[:, res:]
+        for dx in (1, 3, 2):
+            ra_copy(dy, dx).start()
+
+        @pl.when(dy != 0)
+        def _():
+            rb_copy(dy).start()
+
+        @pl.when(b != 0)
+        def _():
+            last = row_offset(b - 1)
+            for dx in (1, 3, 2):
+                ra_copy(last, dx).wait()
+            lrow = (cy + last) % SIDE
+            for r in range(2):
+                total = rsend[lrow, cx, r].astype(F32)
+                for d in range(SIDE - 1):
+                    total = total + ra[lrow, d, r].astype(F32)
+                pasend[last - 1, r] = total.astype(BF16)
+            pa_copy(last).start()
+
         return 0
 
-    lax.fori_loop(0, 4, block_step, 0)
-
-    def r_wait(slot, _):
-        pltpu.make_async_remote_copy(src_ref=rsend.at[0], dst_ref=rrecv.at[slot], send_sem=rs_sem.at[slot], recv_sem=rr_sem.at[slot],
-                                     device_id={'dap': partner}, device_id_type=MESH_ID).wait()
-        return 0
-
-    lax.fori_loop(1, SIDE * SIDE, r_wait, 0)
-    for r in range(rows):
-        acc = lax.fori_loop(1, SIDE * SIDE, lambda s, a: a + rrecv[s, r].astype(F32), rsend[chip, r].astype(F32))
+    lax.fori_loop(0, SIDE, block_step, 0)
+    for d in (1, 3, 2):
+        rb_copy(d).wait()
+
+    def rb_total(x, r):
+        total = rsend[cy, x, 2 + r].astype(F32)
+        for d in range(SIDE - 1):
+            total = total + rb[d, x, r].astype(F32)
+        return total
+
+    for dx in (1, 3, 2):
+        for r in range(2):
+            pbsend[dx - 1, r] = rb_total((cx + dx) % SIDE, r).astype(BF16)
+        pb_copy(dx).start()
+
+    def finish(r, acc):
         term = (acc + bo[...]) / (NORM_EPS + counts[pl.ds(me * rows + r, 1), :])
         mterm = (rmain[r] + mbo[...]) / (NORM_EPS + mcounts[pl.ds(me * rows + r, 1), :])
         out_ref[r] = (z_ref[r] + term.T) + mterm.T
+
+    for dx in (1, 3, 2):
+        ra_copy(0, dx).wait()
+    for dy in (1, 3, 2):
+        pa_copy(dy).wait()
+    for r in range(2):
+        acc = rsend[cy, cx, r].astype(F32)
+        for d in range(SIDE - 1):
+            acc = acc + ra[cy, d, r].astype(F32) + pa[d, r].astype(F32)
+        finish(r, acc)
+    for dx in (1, 3, 2):
+        pb_copy(dx).wait()
+    for r in range(2):
+        acc = rb_total(cx, r)
+        for d in range(SIDE - 1):
+            acc = acc + pb[d, r].astype(F32)
+        finish(2 + r, acc)
 
     def x_wait(k, _):
         pltpu.make_async_remote_copy(src_ref=x_hbm.at[:, :, cols(me)], dst_ref=xb.at[own], send_sem=xs_sem.at[k], recv_sem=xr_sem.at[k],
@@ -390,8 +449,13 @@
             pltpu.VMEM((hidden, res, seqs), BF16),
             pltpu.VMEM((chips, rows * hidden, seqs), BF16),
             pltpu.VMEM((4 * rows, hidden * hidden, res), BF16),
-            pltpu.VMEM((chips, rows, width, res), BF16),
-            pltpu.VMEM((chips, rows, width, res), BF16),
+            pltpu.VMEM((SIDE, SIDE, rows, width, res), BF16),
+            pltpu.VMEM((SIDE, SIDE - 1, rows // 2, width, res), BF16),
+            pltpu.VMEM((SIDE - 1, SIDE, rows // 2, width, res), BF16),
+            pltpu.VMEM((SIDE - 1, rows // 2, width, res), BF16),
+            pltpu.VMEM((SIDE - 1, rows // 2, width, res), BF16),
+            pltpu.VMEM((SIDE - 1, rows // 2, width, res), BF16),
+            pltpu.VMEM((SIDE - 1, rows // 2, width, res), BF16),
             pltpu.VMEM((total, res), jnp.int32),
             pltpu.VMEM((res, seqs), F32),
             pltpu.VMEM((res, res), F32),
@@ -418,8 +482,9 @@
             pltpu.VMEM((rows, width, res), F32),
             pltpu.VMEM((res, mtotal), F32),
             pltpu.VMEM((res, res), F32),
-            dma((devices,)), dma((devices,)), dma((8,)), dma, dma((8,)), dma((8,)), dma((8,)), dma((8,)), dma((chips,)), dma((chips,)),
-            dma((devices,)), dma((devices,)), dma((13,)), dma((13,)),
+            dma((devices,)), dma((devices,)), dma((8,)), dma, dma((8,)), dma((8,)), dma((8,)), dma((8,)),
+            dma((devices,)), dma((devices,)), dma((13,)), dma((13,)), dma((SIDE * (SIDE - 1),)), dma((SIDE * (SIDE - 1),)),
+            dma((SIDE - 1,)), dma((SIDE - 1,)), dma((SIDE - 1,)), dma((SIDE - 1,)), dma((SIDE - 1,)), dma((SIDE - 1,)),
         ],
         compiler_params=pltpu.CompilerParams(collective_id=0, has_side_effects=True, vmem_limit_bytes=60 * 1024 * 1024),
         cost_estimate=pl.CostEstimate(flops=flops, bytes_accessed=20_000_000, transcendentals=0),

time: 158 us -> 144 us (0.911)
  the two profiles are of different devices: /device:TPU:98 before, /device:TPU:112 now
where the time goes in v4:
time: 144 us
  Pallas kernels  132 us (92%)
  local copies, waits for them, and re-layouts  11.3 us (8%)
    pallas_call x1, Pallas kernels, opm_call(): pl.pallas_call(opm_kernel, out_shape=(jax.ShapeDtypeStruct((res, chan, se...  132 us
    unnamed x6, local copies, waits for them, and re-layouts  10.3 us

profile of v4, /device:TPU:112, one launch (start us, length us, event | category | flops | bytes accessed | tf_op | source)
XLA Modules:
  0.0 143.8 jit_solution(5157239383032482955)
XLA Ops:
  0.6 131.9 %opm.1 = (bf16[128,64,384]{2,1,0:T(8,128)(2,1)}, f32[4,128,128]{2,1,0:T(8,128)}, bf16[8,32,4,256]{3,2,1,0:T(4,128)(2,1)}) custom-call(bf16[4,64,12288]{2,1,0:T(8,128)(2,1)} %bitcast.7, s32[12288,128]{1,0:T(8,128)} %mask_hbm.1, bf16[256,4,256]{2,1,0:T(4,128)(2,1)} %main_ref.1, f32[4,128,128]{2,1,0:T(8,128)} %z_ref.1, bf16[64]{0:T(256)(128)(2,1)} %g_in.1, ...), custom_call_target="tpu_custom_call" | custom-call | flops 12884901888 | bytes 20000000 | tf_op jit(solution)/shard_map/opm/pallas_call | solution.py:438
  132.6 0.0 copy-start
  132.6 0.0 copy-start.1
  132.6 9.6 %copy.24 = bf16[384,128,64]{1,2,0:T(8,128)(2,1)} copy(bf16[384,128,64]{0,2,1:T(8,128)(2,1)} %bitcast.6) | data formatting | bytes 12582912
  142.2 0.0 copy-done
  142.2 0.9 reshape.9
  143.1 0.0 copy-done.1
  143.1 0.7 copy.26
Async XLA Ops:
  132.6 9.7 %copy-start = (bf16[8,32,4,256]{3,2,1,0:T(4,128)(2,1)S(1)}, bf16[8,32,4,256]{3,2,1,0:T(4,128)(2,1)}, u32[]{:S(2)}) copy-start(bf16[8,32,4,256]{3,2,1,0:T(4,128)(2,1)} %get-tuple-element.8) | copy-start | bytes 1572868
  132.6 10.6 %copy-start.1 = (f32[4,128,128]{2,1,0:T(8,128)S(1)}, f32[4,128,128]{2,1,0:T(8,128)}, u32[]{:S(2)}) copy-start(f32[4,128,128]{2,1,0:T(8,128)} %get-tuple-element.15) | copy-start | bytes 786436

commit v5 on v4

--- a/solution.py
+++ b/solution.py
@@ -16,6 +16,7 @@
 CORES = 2
 SEND_ORDER = ((1, 1), (3, 3), (1, 3), (3, 1), (2, 2), (2, 1), (0, 2), (2, 3), (0, 1), (0, 3), (1, 2), (2, 0), (3, 2), (1, 0), (3, 0))
 ROW_ORDER = (2, 1, 3, 0)
+EARLY_ROWS = 2
 PAIR_ORDER = ((2, 1), (0, 1), (0, 0), (1, 1), (2, 0), (3, 1), (1, 0), (3, 0))
 
 
@@ -27,7 +28,7 @@
 def opm_kernel(x_hbm, mask_hbm, main_hbm, z_ref, g_in, be_in, wl_in, bl_in, wr_in, br_in, wo_in, bo_in,
                main_ref, mmask, mg_in, mbe_in, mwl_in, mbl_in, mwr_in, mbr_in, mwo_in, mbo_in,
                xout_hbm, out_ref, mout_hbm,
-               xb, xn, aown, apart, bown, bpart, astage, osc, rsend, ra, rb, pasend, pa, pbsend, pb, mraw, maskt, counts,
+               xb, xn, aown, apart, bown, bpart, astage, early, osc, rsend, ra, rb, pasend, pa, pbsend, pb, mraw, maskt, counts,
                akron, bkron, gam, bet, ba, bb, wt, bo, mgam, mbet, mw, mbias, mwt, mbo, wrows,
                mrows, am, perm, gall, bm, rmain, mmaskt, mcounts,
                xs_sem, xr_sem, xo_sem, ms_sem, as_sem, ar_sem, bs_sem, br_sem,
@@ -50,20 +51,30 @@
         return 0
 
     lax.fori_loop(1, SIDE * SIDE * CORES, greet, 0)
-    mask_copy = pltpu.make_async_copy(mask_hbm, mraw, ms_sem)
-    mask_copy.start()
+
+    def mask_copy(k):
+        return pltpu.make_async_copy(mask_hbm.at[pl.ds(k * seqs, seqs)], mraw.at[k % 4], ms_sem.at[k % 4])
+
+    for k in range(3):
+        mask_copy(k).start()
     own = pl.ds(pl.multiple_of(me * rows, rows), rows)
 
-    def cols(p):
-        return pl.ds(pl.multiple_of(p * seqs, 128), seqs)
-
-    pltpu.make_async_copy(x_hbm.at[:, :, cols(me)], xb.at[own], xr_sem.at[0]).start()
+    phases = ((0, seqs - 128), (seqs - 128, 128))
+
+    def cols(p, ph):
+        return pl.ds(pl.multiple_of(p * seqs + phases[ph][0], 128), phases[ph][1])
+
+    def lanes(ph):
+        return pl.ds(*phases[ph])
+
+    for ph in range(2):
+        pltpu.make_async_copy(x_hbm.at[:, :, cols(me, ph)], xb.at[own, :, lanes(ph)], xr_sem.at[ph, 0]).start()
     pl.semaphore_wait(barrier, SIDE * SIDE * CORES - 1)
 
-    def x_copy(dy, dx, dc):
+    def x_copy(dy, dx, dc, ph):
         p = device(dy, dx, dc)
         k = (dy * SIDE + dx) * CORES + dc
-        return pltpu.make_async_remote_copy(src_ref=x_hbm.at[:, :, cols(p)], dst_ref=xb.at[own], send_sem=xs_sem.at[k], recv_sem=xr_sem.at[k],
+        return pltpu.make_async_remote_copy(src_ref=x_hbm.at[:, :, cols(p, ph)], dst_ref=xb.at[own, :, lanes(ph)], send_sem=xs_sem.at[ph, k], recv_sem=xr_sem.at[ph, k],
                                             device_id={'dap': p}, device_id_type=MESH_ID)
 
     mseqs = mout_hbm.shape[0]
@@ -75,14 +86,14 @@
         return pltpu.make_async_remote_copy(src_ref=main_hbm.at[pl.ds(p * mseqs, mseqs)], dst_ref=mout_hbm.at[:, me], send_sem=cs_sem.at[k], recv_sem=cr_sem.at[k],
                                             device_id={'dap': p}, device_id_type=MESH_ID)
 
-    def send(order):
+    def send(order, ph):
         for dy, dx in order:
             for dc in range(CORES):
-                x_copy(dy, dx, dc).start()
-
-    x_copy(0, 0, 1).start()
+                x_copy(dy, dx, dc, ph).start()
+
+    x_copy(0, 0, 1, 0).start()
     pltpu.make_async_copy(main_hbm.at[pl.ds(me * mseqs, mseqs)], mout_hbm.at[:, me], cr_sem.at[0]).start()
-    send(SEND_ORDER[:4])
+    send(SEND_ORDER[:4], 0)
 
     mchan = main_ref.shape[2]
     mgam[...] = mg_in[...].astype(F32).reshape(1, mchan)
@@ -131,7 +142,7 @@
     for d in (1, 3, 2):
         for part in range(2):
             first_copy(part, d).start()
-    send(SEND_ORDER[4:8])
+    send(SEND_ORDER[4:8], 0)
 
     gam[...] = spread(g_in)
     bet[...] = spread(be_in)
@@ -161,16 +172,26 @@
         bkron[:, pl.ds(lt * 128, 128)] = jnp.where(keep, right, 0.0).astype(BF16)
     bb[...] = jnp.broadcast_to(spread(br_in)[:, None, :], (hidden, group, 128)).reshape(hidden * group, 128)
 
-    mask_copy.wait()
     counts[...] = jnp.zeros_like(counts)
+    pieces = SIDE * SIDE * CORES
 
     def count_step(k, _):
-        block = mraw[pl.ds(pl.multiple_of(k * seqs, seqs), seqs), :].astype(F32)
-        counts[...] += jnp.dot(block.T.astype(BF16), block.astype(BF16), preferred_element_type=F32)
-        return 0
-
-    lax.fori_loop(0, mraw.shape[0] // seqs, count_step, 0)
-    maskt[...] = mraw[pl.ds(pl.multiple_of(me * seqs, seqs), seqs), :].astype(F32).T
+        @pl.when(k + 3 < pieces)
+        def _():
+            mask_copy(k + 3).start()
+
+        mask_copy(k).wait()
+        block = mraw[k % 4].astype(F32)
+        turned = block.T
+
+        @pl.when(k == me)
+        def _():
+            maskt[...] = turned
+
+        counts[...] += jnp.dot(turned.astype(BF16), block.astype(BF16), preferred_element_type=F32)
+        return 0
+
+    lax.fori_loop(0, pieces, count_step, 0)
 
     for d in (1, 3, 2):
         for part in range(2):
@@ -178,7 +199,9 @@
     for d in (1, 3, 2):
         for part in range(2):
             second_copy(part, d).start()
-    send(SEND_ORDER[8:])
+    send(SEND_ORDER[8:], 0)
+    x_copy(0, 0, 1, 1).start()
+    send(SEND_ORDER, 1)
 
     partner = device(0, 0, 1)
     qn = 8
@@ -218,20 +241,22 @@
     chip_rows = rows * CORES
     pair_rows = 2 * chip_rows
 
-    def a_copy(u):
-        return pltpu.make_async_remote_copy(src_ref=astage.at[pl.ds(2 * u, 2)], dst_ref=apart.at[pl.ds(2 * u, 2)], send_sem=as_sem.at[u], recv_sem=ar_sem.at[u],
+    def a_copy(u, ph):
+        at = pl.ds(2 * u, 2)
+        return pltpu.make_async_remote_copy(src_ref=astage.at[at, :, lanes(ph)], dst_ref=apart.at[at, :, lanes(ph)], send_sem=as_sem.at[ph, u], recv_sem=ar_sem.at[ph, u],
                                             device_id={'dap': partner}, device_id_type=MESH_ID)
 
-    def b_copy(u):
+    def b_copy(u, ph):
         at = pl.ds(pl.multiple_of(u * pair_rows, pair_rows), pair_rows)
-        return pltpu.make_async_remote_copy(src_ref=bown.at[:, at], dst_ref=bpart.at[:, at], send_sem=bs_sem.at[u], recv_sem=br_sem.at[u],
+        return pltpu.make_async_remote_copy(src_ref=bown.at[:, at, lanes(ph)], dst_ref=bpart.at[:, at, lanes(ph)], send_sem=bs_sem.at[ph, u], recv_sem=br_sem.at[ph, u],
                                             device_id={'dap': partner}, device_id_type=MESH_ID)
 
     def xout_copy(u):
         at = pl.ds(pl.multiple_of(u * pair_rows, pair_rows), pair_rows)
         return pltpu.make_async_copy(xb.at[at], xout_hbm.at[at], xo_sem.at[u])
 
-    def unit_step(pos, _):
+    def unit_step(ph, pos, _):
+        first, width = phases[ph]
         dy = sum((pos == k).astype(jnp.int32) * v for k, (v, _) in enumerate(PAIR_ORDER) if v)
         half = (cx // 2 + sum((pos == k).astype(jnp.int32) for k, (_, v) in enumerate(PAIR_ORDER) if v)) % 2
         ysrc = (cy - dy + SIDE) % SIDE
@@ -240,24 +265,26 @@
             dx = (cx - (2 * half + xx) + SIDE) % SIDE
             for dc in range(CORES):
                 k = (dy * SIDE + dx) * CORES + dc
-                pltpu.make_async_remote_copy(src_ref=xb.at[own], dst_ref=xb.at[own], send_sem=xs_sem.at[k], recv_sem=xr_sem.at[k],
+                here = xb.at[own, :, lanes(ph)]
+                pltpu.make_async_remote_copy(src_ref=here, dst_ref=here, send_sem=xs_sem.at[ph, k], recv_sem=xr_sem.at[ph, k],
                                              device_id={'dap': partner}, device_id_type=MESH_ID).wait_recv()
-        xout_copy(u).start()
-
-        @pl.when(pos == 2)
-        def _():
-            for d in (1, 3, 2):
-                for part in range(2):
-                    second_copy(part, d).wait()
-            last_copy().start()
-
-        @pl.when(pos == 4)
-        def _():
-            main_outer()
+        if ph == 1:
+            xout_copy(u).start()
+        else:
+            @pl.when(pos == 2)
+            def _():
+                for d in (1, 3, 2):
+                    for part in range(2):
+                        second_copy(part, d).wait()
+                last_copy().start()
+
+            @pl.when(pos == 4)
+            def _():
+                main_outer()
 
         def norm_step(n, _):
-            for lt in range(seqs // 128):
-                ls = pl.ds(lt * 128, 128)
+            for lt in range(width // 128):
+                ls = pl.ds(first + lt * 128, 128)
                 v = xb[u * pair_rows + n, :, ls].astype(F32)
                 mean = jnp.sum(v, axis=0, keepdims=True) * (1.0 / chan)
                 d = v - mean
@@ -265,46 +292,65 @@
                 xn[pl.ds(pl.multiple_of(n * chan, chan), chan), ls] = (d * lax.rsqrt(var + LN_EPS) * gam[...] + bet[...]).astype(BF16)
             return 0
 
-        lax.fori_loop(0, pair_rows, norm_step, 0)
+        lax.fori_loop(0, pair_rows, norm_step, 0, unroll=4)
         for k in range(2):
             for dst, cc in ((aown, core), (astage, (core + 1) % CORES)):
                 r0 = k * chip_rows + cc * rows
-                acc = jnp.dot(akron[...], xn[pl.ds(pl.multiple_of(r0 * chan, rows * chan), rows * chan), :], preferred_element_type=F32)
+                acc = jnp.dot(akron[...], xn[pl.ds(pl.multiple_of(r0 * chan, rows * chan), rows * chan), lanes(ph)], preferred_element_type=F32)
                 for r in range(rows):
-                    m = maskt[pl.ds(u * pair_rows + r0 + r, 1), :]
-                    for lt in range(seqs // 128):
+                    m = maskt[pl.ds(u * pair_rows + r0 + r, 1), :][:, first:first + width]
+                    for lt in range(width // 128):
                         ls = slice(lt * 128, lt * 128 + 128)
                         part = (acc[r * hidden:(r + 1) * hidden, ls] + ba[...]) * m[:, ls]
-                        dst[2 * u + k, pl.ds(r * hidden, hidden), pl.ds(lt * 128, 128)] = part.astype(BF16)
-        a_copy(u).start()
+                        dst[2 * u + k, pl.ds(r * hidden, hidden), pl.ds(first + lt * 128, 128)] = part.astype(BF16)
+        a_copy(u, ph).start()
         qc = 16
         for q0 in range(0, hidden, qc):
             parts = []
             for k in range(2):
-                acc = jnp.dot(bkron[pl.ds(q0 * chip_rows, qc * chip_rows), :], xn[pl.ds(k * chip_rows * chan, chip_rows * chan), :], preferred_element_type=F32)
-                m = maskt[pl.ds(pl.multiple_of(u * pair_rows + k * chip_rows, chip_rows), chip_rows), :]
+                acc = jnp.dot(bkron[pl.ds(q0 * chip_rows, qc * chip_rows), :], xn[pl.ds(k * chip_rows * chan, chip_rows * chan), lanes(ph)], preferred_element_type=F32)
+                m = maskt[pl.ds(pl.multiple_of(u * pair_rows + k * chip_rows, chip_rows), chip_rows), lanes(ph)]
                 bias = bb[pl.ds(q0 * chip_rows, qc * chip_rows), :]
-                bias = jnp.concatenate([bias] * (seqs // 128), axis=1)
-                parts.append((acc + bias).reshape(qc, chip_rows, seqs) * m[None])
+                bias = jnp.concatenate([bias] * (width // 128), axis=1)
+                parts.append((acc + bias).reshape(qc, chip_rows, width) * m[None])
             both = jnp.concatenate(parts, axis=1).astype(BF16)
-            bown[pl.ds(q0, qc), pl.ds(pl.multiple_of(u * pair_rows, pair_rows), pair_rows), :] = both
-        b_copy(u).start()
-        return 0
-
-    lax.fori_loop(0, 8, unit_step, 0)
+            bown[pl.ds(q0, qc), pl.ds(pl.multiple_of(u * pair_rows, pair_rows), pair_rows), lanes(ph)] = both
+        b_copy(u, ph).start()
+        return 0
+
+    def exch_wait(ph, u, _):
+        a_copy(u, ph).wait()
+        b_copy(u, ph).wait()
+        if ph == 1:
+            xout_copy(u).wait()
+        return 0
+
+    tall = SIDE * rows * hidden
+
+    def row_offset(b):
+        return sum((b == k).astype(jnp.int32) * v for k, v in enumerate(ROW_ORDER) if v)
+
+    def product(row, qt, qcount, at, width):
+        lhs = jnp.concatenate([ref[pl.ds(row * SIDE, SIDE), :, pl.ds(at, width)].reshape(tall, width) for ref in (aown, apart)], axis=1)
+        rhs = jnp.concatenate([ref[pl.ds(qt * qcount, qcount), :, pl.ds(at, width)].reshape(qcount * res, width) for ref in (bown, bpart)], axis=1)
+        return lax.dot_general(lhs, rhs, (((1,), (1,)), ((), ())), preferred_element_type=F32)
+
+    lax.fori_loop(0, 8, functools.partial(unit_step, 0), 0)
+    lax.fori_loop(0, 8, functools.partial(exch_wait, 0), 0)
+
+    def early_step(k, _):
+        b, qt = k // (hidden // 4), k % (hidden // 4)
+        early[b, qt] = product((cy + row_offset(b)) % SIDE, qt, 4, *phases[0])
+        return 0
+
+    lax.fori_loop(0, EARLY_ROWS * (hidden // 4), early_step, 0)
+    lax.fori_loop(0, 8, functools.partial(unit_step, 1), 0)
 
     main_copy(0, 0, 1).start()
     for dy, dx in SEND_ORDER:
         for dc in range(CORES):
             main_copy(dy, dx, dc).start()
-
-    def exch_wait(u, _):
-        a_copy(u).wait()
-        b_copy(u).wait()
-        xout_copy(u).wait()
-        return 0
-
-    lax.fori_loop(0, 8, exch_wait, 0)
+    lax.fori_loop(0, 8, functools.partial(exch_wait, 1), 0)
 
     def ra_copy(dy, dx):
         row = (cy + dy) % SIDE
@@ -324,33 +370,34 @@
         return pltpu.make_async_remote_copy(src_ref=pbsend.at[dx - 1], dst_ref=pb.at[dx - 1], send_sem=pbs_sem.at[dx - 1], recv_sem=pbr_sem.at[dx - 1],
                                             device_id={'dap': device(0, dx, 0)}, device_id_type=MESH_ID)
 
-    def row_offset(b):
-        return sum((b == k).astype(jnp.int32) * v for k, v in enumerate(ROW_ORDER) if v)
-
-    def block_step(b, _):
+    def block_step(is_early, b, _):
         dy = row_offset(b)
         row = (cy + dy) % SIDE
-        tall = SIDE * rows * hidden
 
         def q_step(qt, _):
-            lhs = jnp.concatenate([ref[pl.ds(row * SIDE, SIDE)].reshape(tall, seqs) for ref in (aown, apart)], axis=1)
-            rhs = jnp.concatenate([ref[pl.ds(qt * qn, qn)].reshape(qn * res, seqs) for ref in (bown, bpart)], axis=1)
-            prod = lax.dot_general(lhs, rhs, (((1,), (1,)), ((), ())), preferred_element_type=F32).astype(BF16)
+            if is_early:
+                prod = product(row, qt, 4, *phases[1])
+                prod = (prod + early[b, qt]).astype(BF16)
+                qcount = 4
+            else:
+                prod = product(row, qt, qn, 0, seqs).astype(BF16)
+                qcount = qn
             for i in range(SIDE * rows):
-                for q in range(qn):
-                    osc[i, pl.ds(pl.multiple_of(qt * (qn * hidden) + q * hidden, hidden), hidden), :] = prod[i * hidden:(i + 1) * hidden, q * res:(q + 1) * res]
+                for q in range(qcount):
+                    osc[i, pl.ds(pl.multiple_of(qt * (qcount * hidden) + q * hidden, hidden), hidden), :] = prod[i * hidden:(i + 1) * hidden, q * res:(q + 1) * res]
             return 0
 
-        lax.fori_loop(0, hidden // qn, q_step, 0)
-        for t in range(SIDE):
-            for r in range(0, rows, 2):
+        lax.fori_loop(0, hidden // (4 if is_early else qn), q_step, 0)
+        for r in range(0, rows, 2):
+            for t in range(SIDE):
                 i = t * rows + r
                 rhs = jnp.concatenate([osc[i], osc[i + 1]], axis=1)
                 pair = jnp.dot(wt[...], rhs, preferred_element_type=F32).astype(BF16)
                 rsend[row, t, r] = pair[:, :res]
                 rsend[row, t, r + 1] = pair[:, res:]
-        for dx in (1, 3, 2):
-            ra_copy(dy, dx).start()
+            if r == 0:
+                for dx in (1, 3, 2):
+                    ra_copy(dy, dx).start()
 
         @pl.when(dy != 0)
         def _():
@@ -371,7 +418,8 @@
 
         return 0
 
-    lax.fori_loop(0, SIDE, block_step, 0)
+    lax.fori_loop(0, EARLY_ROWS, functools.partial(block_step, True), 0)
+    lax.fori_loop(EARLY_ROWS, SIDE, functools.partial(block_step, False), 0)
     for d in (1, 3, 2):
         rb_copy(d).wait()
 
@@ -409,8 +457,9 @@
         finish(2 + r, acc)
 
     def x_wait(k, _):
-        pltpu.make_async_remote_copy(src_ref=x_hbm.at[:, :, cols(me)], dst_ref=xb.at[own], send_sem=xs_sem.at[k], recv_sem=xr_sem.at[k],
-                                     device_id={'dap': partner}, device_id_type=MESH_ID).wait_send()
+        for ph in range(2):
+            pltpu.make_async_remote_copy(src_ref=x_hbm.at[:, :, cols(me, ph)], dst_ref=xb.at[own, :, lanes(ph)], send_sem=xs_sem.at[ph, k], recv_sem=xr_sem.at[ph, k],
+                                         device_id={'dap': partner}, device_id_type=MESH_ID).wait_send()
         pltpu.make_async_remote_copy(src_ref=main_hbm.at[pl.ds(0, mseqs)], dst_ref=mout_hbm.at[:, me], send_sem=cs_sem.at[k], recv_sem=cr_sem.at[k],
                                      device_id={'dap': partner}, device_id_type=MESH_ID).wait()
         return 0
@@ -448,6 +497,7 @@
             pltpu.VMEM((hidden, res, seqs), BF16),
             pltpu.VMEM((hidden, res, seqs), BF16),
             pltpu.VMEM((chips, rows * hidden, seqs), BF16),
+            pltpu.VMEM((EARLY_ROWS, hidden // 4, SIDE * rows * hidden, 4 * res), F32),
             pltpu.VMEM((4 * rows, hidden * hidden, res), BF16),
             pltpu.VMEM((SIDE, SIDE, rows, width, res), BF16),
             pltpu.VMEM((SIDE, SIDE - 1, rows // 2, width, res), BF16),
@@ -456,7 +506,7 @@
             pltpu.VMEM((SIDE - 1, rows // 2, width, res), BF16),
             pltpu.VMEM((SIDE - 1, rows // 2, width, res), BF16),
             pltpu.VMEM((SIDE - 1, rows // 2, width, res), BF16),
-            pltpu.VMEM((total, res), jnp.int32),
+            pltpu.VMEM((4, seqs, res), jnp.int32),
             pltpu.VMEM((res, seqs), F32),
             pltpu.VMEM((res, res), F32),
             pltpu.VMEM((rows * hidden, rows * chan), BF16),
@@ -482,11 +532,11 @@
             pltpu.VMEM((rows, width, res), F32),
             pltpu.VMEM((res, mtotal), F32),
             pltpu.VMEM((res, res), F32),
-            dma((devices,)), dma((devices,)), dma((8,)), dma, dma((8,)), dma((8,)), dma((8,)), dma((8,)),
+            dma((2, devices)), dma((2, devices)), dma((8,)), dma((4,)), dma((2, 8)), dma((2, 8)), dma((2, 8)), dma((2, 8)),
             dma((devices,)), dma((devices,)), dma((13,)), dma((13,)), dma((SIDE * (SIDE - 1),)), dma((SIDE * (SIDE - 1),)),
             dma((SIDE - 1,)), dma((SIDE - 1,)), dma((SIDE - 1,)), dma((SIDE - 1,)), dma((SIDE - 1,)), dma((SIDE - 1,)),
         ],
-        compiler_params=pltpu.CompilerParams(collective_id=0, has_side_effects=True, vmem_limit_bytes=60 * 1024 * 1024),
+        compiler_params=pltpu.CompilerParams(collective_id=0, has_side_effects=True, vmem_limit_bytes=62 * 1024 * 1024),
         cost_estimate=pl.CostEstimate(flops=flops, bytes_accessed=20_000_000, transcendentals=0),
         name='opm',
     )(x, mask, main, z, ln_gamma, ln_beta, w_left.T, b_left, w_right.T, b_right, w_out, b_out,

time: 144 us -> 141 us (0.979)
  the two profiles are of different devices: /device:TPU:112 before, /device:TPU:98 now
where the time goes in v5:
time: 141 us; the launch traced here: 140 us
  Pallas kernels  128 us (91%)
  local copies, waits for them, and re-layouts  11.3 us (8%)
    pallas_call x1, Pallas kernels, opm_call(): pl.pallas_call(opm_kernel, out_shape=(jax.ShapeDtypeStruct((res, chan, se...  128 us
    unnamed x6, local copies, waits for them, and re-layouts  10.3 us

profile of v5, /device:TPU:98, one launch (start us, length us, event | category | flops | bytes accessed | tf_op | source)
XLA Modules:
  0.0 140.2 jit_solution(17250698805999249586)
XLA Ops:
  0.6 128.3 %opm.1 = (bf16[128,64,384]{2,1,0:T(8,128)(2,1)}, f32[4,128,128]{2,1,0:T(8,128)}, bf16[8,32,4,256]{3,2,1,0:T(4,128)(2,1)}) custom-call(bf16[4,64,12288]{2,1,0:T(8,128)(2,1)} %bitcast.7, s32[12288,128]{1,0:T(8,128)} %mask_hbm.1, bf16[256,4,256]{2,1,0:T(4,128)(2,1)} %main_ref.1, f32[4,128,128]{2,1,0:T(8,128)} %z_ref.1, bf16[64]{0:T(256)(128)(2,1)} %g_in.1, ...), custom_call_target="tpu_custom_call" | custom-call | flops 12884901888 | bytes 20000000 | tf_op jit(solution)/shard_map/opm/pallas_call | solution.py:487
  128.9 0.0 copy-start
  128.9 0.0 copy-start.1
  128.9 9.6 %copy.24 = bf16[384,128,64]{1,2,0:T(8,128)(2,1)} copy(bf16[384,128,64]{0,2,1:T(8,128)(2,1)} %bitcast.6) | data formatting | bytes 12582912
  138.6 0.0 copy-done
  138.6 0.9 reshape.9
  139.5 0.0 copy-done.1
  139.5 0.7 copy.26
Async XLA Ops:
  128.9 9.7 %copy-start = (bf16[8,32,4,256]{3,2,1,0:T(4,128)(2,1)S(1)}, bf16[8,32,4,256]{3,2,1,0:T(4,128)(2,1)}, u32[]{:S(2)}) copy-start(bf16[8,32,4,256]{3,2,1,0:T(4,128)(2,1)} %get-tuple-element.8) | copy-start | bytes 1572868
  128.9 10.6 %copy-start.1 = (f32[4,128,128]{2,1,0:T(8,128)S(1)}, f32[4,128,128]{2,1,0:T(8,128)}, u32[]{:S(2)}) copy-start(f32[4,128,128]{2,1,0:T(8,128)} %get-tuple-element.15) | copy-start | bytes 786436

commit v6 on v5

--- a/solution.py
+++ b/solution.py
@@ -16,7 +16,7 @@
 CORES = 2
 SEND_ORDER = ((1, 1), (3, 3), (1, 3), (3, 1), (2, 2), (2, 1), (0, 2), (2, 3), (0, 1), (0, 3), (1, 2), (2, 0), (3, 2), (1, 0), (3, 0))
 ROW_ORDER = (2, 1, 3, 0)
-EARLY_ROWS = 2
+EARLY_ROWS = 3
 PAIR_ORDER = ((2, 1), (0, 1), (0, 0), (1, 1), (2, 0), (3, 1), (1, 0), (3, 0))
 
 
@@ -50,7 +50,7 @@
         pl.semaphore_signal(barrier, inc=1, device_id={'dap': (me + k) % (SIDE * SIDE * CORES)}, device_id_type=MESH_ID)
         return 0
 
-    lax.fori_loop(1, SIDE * SIDE * CORES, greet, 0)
+    lax.fori_loop(1, SIDE * SIDE * CORES, greet, 0, unroll=True)
 
     def mask_copy(k):
         return pltpu.make_async_copy(mask_hbm.at[pl.ds(k * seqs, seqs)], mraw.at[k % 4], ms_sem.at[k % 4])
@@ -235,8 +235,9 @@
         lax.fori_loop(0, hidden // qn, q_step, 0)
         for r in range(0, rows, 2):
             pair = jnp.dot(mwt[...], jnp.concatenate([osc[r], osc[r + 1]], axis=1), preferred_element_type=F32)
-            rmain[r] = pair[:, :res]
-            rmain[r + 1] = pair[:, res:]
+            for k in range(2):
+                total = pair[:, k * res:(k + 1) * res]
+                rmain[r + k] = ((total + mbo[...]) / (NORM_EPS + mcounts[pl.ds(me * rows + r + k, 1), :])).T
 
     chip_rows = rows * CORES
     pair_rows = 2 * chip_rows
@@ -339,11 +340,11 @@
     lax.fori_loop(0, 8, functools.partial(exch_wait, 0), 0)
 
     def early_step(k, _):
-        b, qt = k // (hidden // 4), k % (hidden // 4)
-        early[b, qt] = product((cy + row_offset(b)) % SIDE, qt, 4, *phases[0])
-        return 0
-
-    lax.fori_loop(0, EARLY_ROWS * (hidden // 4), early_step, 0)
+        b, qt = k // (hidden // qn), k % (hidden // qn)
+        early[b, qt] = product((cy + row_offset(b)) % SIDE, qt, qn, *phases[0])
+        return 0
+
+    lax.fori_loop(0, EARLY_ROWS * (hidden // qn), early_step, 0)
     lax.fori_loop(0, 8, functools.partial(unit_step, 1), 0)
 
     main_copy(0, 0, 1).start()
@@ -376,18 +377,15 @@
 
         def q_step(qt, _):
             if is_early:
-                prod = product(row, qt, 4, *phases[1])
-                prod = (prod + early[b, qt]).astype(BF16)
-                qcount = 4
+                prod = (product(row, qt, qn, *phases[1]) + early[b, qt]).astype(BF16)
             else:
                 prod = product(row, qt, qn, 0, seqs).astype(BF16)
-                qcount = qn
             for i in range(SIDE * rows):
-                for q in range(qcount):
-                    osc[i, pl.ds(pl.multiple_of(qt * (qcount * hidden) + q * hidden, hidden), hidden), :] = prod[i * hidden:(i + 1) * hidden, q * res:(q + 1) * res]
+                for q in range(qn):
+                    osc[i, pl.ds(pl.multiple_of(qt * (qn * hidden) + q * hidden, hidden), hidden), :] = prod[i * hidden:(i + 1) * hidden, q * res:(q + 1) * res]
             return 0
 
-        lax.fori_loop(0, hidden // (4 if is_early else qn), q_step, 0)
+        lax.fori_loop(0, hidden // qn, q_step, 0)
         for r in range(0, rows, 2):
             for t in range(SIDE):
                 i = t * rows + r
@@ -436,9 +434,18 @@
 
     def finish(r, acc):
         term = (acc + bo[...]) / (NORM_EPS + counts[pl.ds(me * rows + r, 1), :])
-        mterm = (rmain[r] + mbo[...]) / (NORM_EPS + mcounts[pl.ds(me * rows + r, 1), :])
-        out_ref[r] = (z_ref[r] + term.T) + mterm.T
-
+        out_ref[r] = (z_ref[r] + term.T) + rmain[r]
+
+    def x_wait(k, _):
+        for ph in range(2):
+            pltpu.make_async_remote_copy(src_ref=x_hbm.at[:, :, cols(me, ph)], dst_ref=xb.at[own, :, lanes(ph)], send_sem=xs_sem.at[ph, k], recv_sem=xr_sem.at[ph, k],
+                                         device_id={'dap': partner}, device_id_type=MESH_ID).wait_send()
+        pltpu.make_async_remote_copy(src_ref=main_hbm.at[pl.ds(0, mseqs)], dst_ref=mout_hbm.at[:, me], send_sem=cs_sem.at[k], recv_sem=cr_sem.at[k],
+                                     device_id={'dap': partner}, device_id_type=MESH_ID).wait()
+        return 0
+
+    lax.fori_loop(1, SIDE * SIDE * CORES, x_wait, 0)
+    pltpu.make_async_copy(main_hbm.at[pl.ds(me * mseqs, mseqs)], mout_hbm.at[:, me], cr_sem.at[0]).wait()
     for dx in (1, 3, 2):
         ra_copy(0, dx).wait()
     for dy in (1, 3, 2):
@@ -455,17 +462,6 @@
         for d in range(SIDE - 1):
             acc = acc + pb[d, r].astype(F32)
         finish(2 + r, acc)
-
-    def x_wait(k, _):
-        for ph in range(2):
-            pltpu.make_async_remote_copy(src_ref=x_hbm.at[:, :, cols(me, ph)], dst_ref=xb.at[own, :, lanes(ph)], send_sem=xs_sem.at[ph, k], recv_sem=xr_sem.at[ph, k],
-                                         device_id={'dap': partner}, device_id_type=MESH_ID).wait_send()
-        pltpu.make_async_remote_copy(src_ref=main_hbm.at[pl.ds(0, mseqs)], dst_ref=mout_hbm.at[:, me], send_sem=cs_sem.at[k], recv_sem=cr_sem.at[k],
-                                     device_id={'dap': partner}, device_id_type=MESH_ID).wait()
-        return 0
-
-    lax.fori_loop(1, SIDE * SIDE * CORES, x_wait, 0)
-    pltpu.make_async_copy(main_hbm.at[pl.ds(me * mseqs, mseqs)], mout_hbm.at[:, me], cr_sem.at[0]).wait()
 
 
 def opm_call(x, mask, z, main, mmask, extra_weights, main_weights):
@@ -497,7 +493,7 @@
             pltpu.VMEM((hidden, res, seqs), BF16),
             pltpu.VMEM((hidden, res, seqs), BF16),
             pltpu.VMEM((chips, rows * hidden, seqs), BF16),
-            pltpu.VMEM((EARLY_ROWS, hidden // 4, SIDE * rows * hidden, 4 * res), F32),
+            pltpu.VMEM((EARLY_ROWS, hidden // 8, SIDE * rows * hidden, 8 * res), F32),
             pltpu.VMEM((4 * rows, hidden * hidden, res), BF16),
             pltpu.VMEM((SIDE, SIDE, rows, width, res), BF16),
             pltpu.VMEM((SIDE, SIDE - 1, rows // 2, width, res), BF16),
@@ -529,7 +525,7 @@
             pltpu.VMEM((2 * chip_rows * hidden, 2 * chip_rows * hidden), BF16),
             pltpu.VMEM((CORES, SIDE, SIDE, 2, rows // 2 * hidden, mtotal), BF16),
             pltpu.VMEM((hidden, res, mtotal), BF16),
-            pltpu.VMEM((rows, width, res), F32),
+            pltpu.VMEM((rows, res, width), F32),
             pltpu.VMEM((res, mtotal), F32),
             pltpu.VMEM((res, res), F32),
             dma((2, devices)), dma((2, devices)), dma((8,)), dma((4,)), dma((2, 8)), dma((2, 8)), dma((2, 8)), dma((2, 8)),

time: 141 us -> 137 us (0.972)
  Pallas kernels: 128 us -> 125 us
    pallas_call x1, Pallas kernels: 128 us -> 125 us  [opm_call(): pl.pallas_call(opm_kernel, out_shape=(jax.ShapeDtypeStruct((res, chan, se...]
where the time goes in v6:
time: 137 us
  Pallas kernels  125 us (91%)
  local copies, waits for them, and re-layouts  11.3 us (8%)
    pallas_call x1, Pallas kernels, opm_call(): pl.pallas_call(opm_kernel, out_shape=(jax.ShapeDtypeStruct((res, chan, se...  125 us
    unnamed x6, local copies, waits for them, and re-layouts  10.3 us

profile of v6, /device:TPU:98, one launch (start us, length us, event | category | flops | bytes accessed | tf_op | source)
XLA Modules:
  0.0 136.8 jit_solution(17965221078232803854)
XLA Ops:
  0.6 124.9 %opm.1 = (bf16[128,64,384]{2,1,0:T(8,128)(2,1)}, f32[4,128,128]{2,1,0:T(8,128)}, bf16[8,32,4,256]{3,2,1,0:T(4,128)(2,1)}) custom-call(bf16[4,64,12288]{2,1,0:T(8,128)(2,1)} %bitcast.7, s32[12288,128]{1,0:T(8,128)} %mask_hbm.1, bf16[256,4,256]{2,1,0:T(4,128)(2,1)} %main_ref.1, f32[4,128,128]{2,1,0:T(8,128)} %z_ref.1, bf16[64]{0:T(256)(128)(2,1)} %g_in.1, ...), custom_call_target="tpu_custom_call" | custom-call | flops 12884901888 | bytes 20000000 | tf_op jit(solution)/shard_map/opm/pallas_call | solution.py:483
  125.6 0.0 copy-start
  125.6 0.0 copy-start.1
  125.6 9.6 %copy.24 = bf16[384,128,64]{1,2,0:T(8,128)(2,1)} copy(bf16[384,128,64]{0,2,1:T(8,128)(2,1)} %bitcast.6) | data formatting | bytes 12582912
  135.2 0.0 copy-done
  135.2 0.9 reshape.9
  136.1 0.0 copy-done.1
  136.1 0.7 copy.26
Async XLA Ops:
  125.6 9.7 %copy-start = (bf16[8,32,4,256]{3,2,1,0:T(4,128)(2,1)S(1)}, bf16[8,32,4,256]{3,2,1,0:T(4,128)(2,1)}, u32[]{:S(2)}) copy-start(bf16[8,32,4,256]{3,2,1,0:T(4,128)(2,1)} %get-tuple-element.8) | copy-start | bytes 1572868
  125.6 10.6 %copy-start.1 = (f32[4,128,128]{2,1,0:T(8,128)S(1)}, f32[4,128,128]{2,1,0:T(8,128)}, u32[]{:S(2)}) copy-start(f32[4,128,128]{2,1,0:T(8,128)} %get-tuple-element.15) | copy-start | bytes 786436

commit v7 on v6

--- a/solution.py
+++ b/solution.py
@@ -261,6 +261,14 @@
         dy = sum((pos == k).astype(jnp.int32) * v for k, (v, _) in enumerate(PAIR_ORDER) if v)
         half = (cx // 2 + sum((pos == k).astype(jnp.int32) for k, (_, v) in enumerate(PAIR_ORDER) if v)) % 2
         ysrc = (cy - dy + SIDE) % SIDE
+        if ph == 1:
+            @pl.when(pos == 6)
+            def _():
+                main_copy(0, 0, 1).start()
+                for ddy, ddx in SEND_ORDER:
+                    for dc in range(CORES):
+                        main_copy(ddy, ddx, dc).start()
+
         u = ysrc * 2 + half
         for xx in range(2):
             dx = (cx - (2 * half + xx) + SIDE) % SIDE
@@ -320,10 +328,15 @@
         return 0
 
     def exch_wait(ph, u, _):
-        a_copy(u, ph).wait()
-        b_copy(u, ph).wait()
-        if ph == 1:
-            xout_copy(u).wait()
+        a_copy(u, ph).wait_recv()
+        b_copy(u, ph).wait_recv()
+        return 0
+
+    def sent_wait(u, _):
+        for ph in range(2):
+            a_copy(u, ph).wait_send()
+            b_copy(u, ph).wait_send()
+        xout_copy(u).wait()
         return 0
 
     tall = SIDE * rows * hidden
@@ -337,7 +350,7 @@
         return lax.dot_general(lhs, rhs, (((1,), (1,)), ((), ())), preferred_element_type=F32)
 
     lax.fori_loop(0, 8, functools.partial(unit_step, 0), 0)
-    lax.fori_loop(0, 8, functools.partial(exch_wait, 0), 0)
+    lax.fori_loop(0, 8, functools.partial(exch_wait, 0), 0, unroll=True)
 
     def early_step(k, _):
         b, qt = k // (hidden // qn), k % (hidden // qn)
@@ -347,11 +360,7 @@
     lax.fori_loop(0, EARLY_ROWS * (hidden // qn), early_step, 0)
     lax.fori_loop(0, 8, functools.partial(unit_step, 1), 0)
 
-    main_copy(0, 0, 1).start()
-    for dy, dx in SEND_ORDER:
-        for dc in range(CORES):
-            main_copy(dy, dx, dc).start()
-    lax.fori_loop(0, 8, functools.partial(exch_wait, 1), 0)
+    lax.fori_loop(0, 8, functools.partial(exch_wait, 1), 0, unroll=True)
 
     def ra_copy(dy, dx):
         row = (cy + dy) % SIDE
@@ -445,6 +454,7 @@
         return 0
 
     lax.fori_loop(1, SIDE * SIDE * CORES, x_wait, 0)
+    lax.fori_loop(0, 8, sent_wait, 0)
     pltpu.make_async_copy(main_hbm.at[pl.ds(me * mseqs, mseqs)], mout_hbm.at[:, me], cr_sem.at[0]).wait()
     for dx in (1, 3, 2):
         ra_copy(0, dx).wait()

time: 137 us -> 137 us (level); the launches traced: 137 us -> 134 us
  Pallas kernels: 125 us -> 122 us
    pallas_call x1, Pallas kernels: 125 us -> 122 us  [opm_call(): pl.pallas_call(opm_kernel, out_shape=(jax.ShapeDtypeStruct((res, chan, se...]
where the time goes in v7:
time: 137 us; the launch traced here: 134 us
  Pallas kernels  122 us (89%)
  local copies, waits for them, and re-layouts  11.3 us (8%)
    pallas_call x1, Pallas kernels, opm_call(): pl.pallas_call(opm_kernel, out_shape=(jax.ShapeDtypeStruct((res, chan, se...  122 us
    unnamed x6, local copies, waits for them, and re-layouts  10.3 us

profile of v7, /device:TPU:98, one launch (start us, length us, event | category | flops | bytes accessed | tf_op | source)
XLA Modules:
  0.0 134.0 jit_solution(6429561990403798326)
XLA Ops:
  0.6 122.1 %opm.1 = (bf16[128,64,384]{2,1,0:T(8,128)(2,1)}, f32[4,128,128]{2,1,0:T(8,128)}, bf16[8,32,4,256]{3,2,1,0:T(4,128)(2,1)}) custom-call(bf16[4,64,12288]{2,1,0:T(8,128)(2,1)} %bitcast.7, s32[12288,128]{1,0:T(8,128)} %mask_hbm.1, bf16[256,4,256]{2,1,0:T(4,128)(2,1)} %main_ref.1, f32[4,128,128]{2,1,0:T(8,128)} %z_ref.1, bf16[64]{0:T(256)(128)(2,1)} %g_in.1, ...), custom_call_target="tpu_custom_call" | custom-call | flops 12884901888 | bytes 20000000 | tf_op jit(solution)/shard_map/opm/pallas_call | solution.py:493
  122.8 0.0 copy-start
  122.8 0.0 copy-start.1
  122.8 9.6 %copy.24 = bf16[384,128,64]{1,2,0:T(8,128)(2,1)} copy(bf16[384,128,64]{0,2,1:T(8,128)(2,1)} %bitcast.6) | data formatting | bytes 12582912
  132.4 0.0 copy-done
  132.4 0.9 reshape.9
  133.3 0.0 copy-done.1
  133.3 0.7 copy.26
Async XLA Ops:
  122.8 9.7 %copy-start = (bf16[8,32,4,256]{3,2,1,0:T(4,128)(2,1)S(1)}, bf16[8,32,4,256]{3,2,1,0:T(4,128)(2,1)}, u32[]{:S(2)}) copy-start(bf16[8,32,4,256]{3,2,1,0:T(4,128)(2,1)} %get-tuple-element.8) | copy-start | bytes 1572868
  122.8 10.6 %copy-start.1 = (f32[4,128,128]{2,1,0:T(8,128)S(1)}, f32[4,128,128]{2,1,0:T(8,128)}, u32[]{:S(2)}) copy-start(f32[4,128,128]{2,1,0:T(8,128)} %get-tuple-element.15) | copy-start | bytes 786436
